TPU v7x, 32 devices: a whole 2x2x4 slice. The times are simulated.
32 devices in a mesh: dp: 8 (over z, x), cent: 4 (over y, core).
Axes of the slice: x: 2, y: 2, z: 4, core: 2. Of those that a mesh axis runs over, the one named last changes fastest.
Arguments:
- documents: bfloat16 [16384, 2048], P(('dp', 'cent')), may hold values from -6 to 6
- assigned: int32 [16384], P(('dp', 'cent')), may hold values from 0 to 12287, as said below
- centroids: bfloat16 [12288, 2048], P(('dp', 'cent')), may hold values from -6 to 6
- owner_slot: int32 [12288], replicated, may hold values from 0 to 12287, as said below
Outputs:
- prototypicality: float32 [16384], P(('dp', 'cent'))
- redundancy: float32 [16384], P(('dp', 'cent'))
- cluster_stats: float32 [3, 12288], P(None, ('dp', 'cent'))
Inputs may be any that keep to these rules, and one draw needn't show every extreme that they name: `owner_slot`: A permutation of the cluster numbers. `assigned`: of the 512 documents of one device, at most 32 have a slot in any one owner's block of 384 slots, and at most 80 have slots with the owners that share one dp index; in every draw some device reaches 80, and one owner receives exactly 32 from every device.
All inputs are finite; a program needn't handle non-finite values.
Results may differ from a plain program's by a relative error of at most 0.0003.
Values may be sent and summed in bfloat16 or wider, within the bound.
A program may use at most 64 MiB of HBM per device.

v0:
```python
import functools
import math

import jax
import jax.numpy as jnp
from jax import lax
from jax.experimental import pallas as pl
from jax.experimental.pallas import tpu as pltpu
from jax.sharding import PartitionSpec as P

F32 = jnp.float32
BF16 = jnp.bfloat16
HIGH = lax.Precision.HIGHEST
LANES = 128
SUB = 8


def round_up(value, unit):
    return -(-value // unit) * unit


def each(low, high, body):
    if high - low <= 8:
        for step in range(low, high):
            body(step)
    else:
        lax.fori_loop(low, high, lambda step, carry: (body(step), carry)[1], 0)


def iota(shape, dim):
    return lax.broadcasted_iota(jnp.int32, shape, dim)


def mm(left, right):
    return lax.dot_general(left, right, (((1,), (0,)), ((), ())), preferred_element_type=F32)


def mm_t(left, right):
    return lax.dot_general(left, right, (((1,), (1,)), ((), ())), preferred_element_type=F32)


def one_hot(condition):
    return jnp.where(condition, 1.0, 0.0).astype(BF16)


def kernel(
    dims,
    docs_ref,
    assigned_ref,
    cent_ref,
    table_ref,
    out_ref,
    send_buf,
    chunk_buf,
    code_send,
    code_recv,
    fwd_buf,
    rows_buf,
    tbl_send,
    tbl_recv,
    res_send,
    res_recv,
    tag_col,
    tag_row,
    inv_col,
    inv_row,
    sim_col,
    best_row,
    a_send,
    a_recv,
    m_send,
    m_recv,
    f_send,
    f_recv,
    t_send,
    t_recv,
    r_send,
    r_recv,
    stats_ref,
):
    R, C, K, Q = dims
    O = R * C
    CK = C * K
    L, D = docs_ref.shape
    S = cent_ref.shape[0]
    T = table_ref.shape[0]
    row_me = lax.axis_index("dp")
    col_me = lax.axis_index("cent")
    own = row_me * C + col_me

    bits = []
    while 2 ** len(bits) < R:
        bits.append(lax.rem(lax.div(row_me, 2 ** len(bits)), 2))
    col_of = [col_me] + [lax.rem(col_me + d, C) for d in range(1, C)]

    def row_of(t):
        total = 0
        for i, bit in enumerate(bits):
            if isinstance(t, int):
                total = total + (1 - bit if (t >> i) & 1 else bit) * 2**i
            else:
                total = total + lax.rem(bit + lax.div(t, 2**i), 2) * 2**i
        return total

    def all_peers(body):
        for d in range(1, C):
            body(0, row_me, d)

        def at_row(t):
            r = row_of(t)
            for d in range(C):
                body(t, r, d)

        each(1, R, at_row)

    def where_is(r, c):
        return {"dp": r, "cent": c}

    def remote(src, dst, send, recv, r, c):
        return pltpu.make_async_remote_copy(
            src_ref=src,
            dst_ref=dst,
            send_sem=send,
            recv_sem=recv,
            device_id=where_is(r, c),
            device_id_type=pl.DeviceIdType.MESH,
        )

    barrier = pltpu.get_barrier_semaphore()

    def greet(t, r, d):
        pl.semaphore_signal(
            barrier, inc=1, device_id=where_is(r, col_of[d]), device_id_type=pl.DeviceIdType.MESH
        )

    all_peers(greet)

    assigned = assigned_ref[...]
    high = lax.shift_right_logical(assigned, 7)
    low = jnp.bitwise_and(assigned, 127)
    table = table_ref[...]
    d0 = jnp.bitwise_and(table, 127)
    d1 = jnp.bitwise_and(lax.shift_right_logical(table, 7), 127)
    d2 = lax.shift_right_logical(table, 14)
    pick = one_hot(iota((T, L), 0) == high)

    def look(digit):
        return lax.dot_general(
            digit.astype(F32).astype(BF16), pick, (((0,), (0,)), ((), ())), preferred_element_type=F32
        )

    looked = look(d0) + 128.0 * look(d1) + 16384.0 * look(d2)
    slot = jnp.sum(jnp.where(iota((LANES, L), 0) == low, looked, 0.0), axis=0, keepdims=True)
    owner = jnp.floor((slot + 0.5) * (1.0 / S))
    local_id = slot - owner * S
    row = jnp.floor((owner + 0.5) * (1.0 / C))
    owner_i = owner.astype(jnp.int32)
    row_i = row.astype(jnp.int32)
    is_owner = jnp.where(iota((O, L), 0) == owner_i, 1.0, 0.0)
    is_row = jnp.where(iota((R, L), 0) == row_i, 1.0, 0.0)
    earlier = one_hot(iota((L, L), 0) < iota((L, L), 1))
    rank_owner = jnp.sum(mm(is_owner.astype(BF16), earlier) * is_owner, axis=0, keepdims=True)
    rank_row = jnp.sum(mm(is_row.astype(BF16), earlier) * is_row, axis=0, keepdims=True)
    position = jnp.bitwise_xor(row_i, row_me) * Q + rank_row.astype(jnp.int32)
    code = ((owner - row * C) * K + rank_owner + 1.0).astype(BF16)
    code8 = jnp.broadcast_to(code, (SUB, L))
    rank_i = rank_owner.astype(jnp.int32)
    docs = docs_ref[...]

    is_owner8 = lax.shift_right_logical(iota((O * SUB, L), 0), 3) == owner_i
    is_rank = one_hot(iota((LANES, L), 0) == rank_i)
    tag = local_id + 1.0
    tag_hi = jnp.floor(tag * (1.0 / 128.0))
    tag_lo = tag - tag_hi * 128.0
    tags = 128.0 * mm_t(jnp.where(is_owner8, tag_hi, 0.0).astype(BF16), is_rank) + mm_t(
        jnp.where(is_owner8, tag_lo, 0.0).astype(BF16), is_rank
    )
    tbl_send[...] = tags.reshape(O, SUB, LANES)

    pl.semaphore_wait(barrier, O - 1)

    def tbl_copy(t, r, d):
        return remote(
            tbl_send.at[r * C + col_of[d]],
            tbl_recv.at[t * C + col_me],
            t_send.at[t * C + d],
            t_recv.at[t * C + col_me],
            r,
            col_of[d],
        )

    def tbl_arrival(t, r, d):
        return remote(
            tbl_send.at[r * C + col_of[d]],
            tbl_recv.at[t * C + col_of[d]],
            t_send.at[t * C + d],
            t_recv.at[t * C + col_of[d]],
            r,
            col_of[d],
        )

    all_peers(lambda t, r, d: tbl_copy(t, r, d).start())
    tbl_recv[col_me] = tbl_send[own]

    def row_copy(t, r):
        return remote(send_buf.at[t], chunk_buf.at[t], a_send.at[t], a_recv.at[t], r, col_me)

    def code_copy(t, r):
        return remote(code_send.at[t], code_recv.at[t], m_send.at[t], m_recv.at[t], r, col_me)

    def mark(t):
        code_send[t] = mm_t(code8, one_hot(iota((Q, L), 0) + t * Q == position))

    each(0, R, mark)
    each(1, R, lambda t: code_copy(t, row_of(t)).start())
    code_recv[0] = code_send[0]

    group = max(1, R // 2)
    for first in range(0, R, group):
        choose = one_hot(iota((group * Q, L), 0) + first * Q == position)
        send_buf[first : first + group] = mm(choose, docs).astype(BF16).reshape(group, Q, D)
        each(max(first, 1), first + group, lambda t: row_copy(t, row_of(t)).start())
    chunk_buf[0] = send_buf[0]

    def fwd_copy(t, c):
        return remote(
            fwd_buf.at[t, c], rows_buf.at[t, col_me], f_send.at[t, c], f_recv.at[t, col_me], row_me, c
        )

    def fwd_arrival(t, c):
        return remote(fwd_buf.at[t, c], rows_buf.at[t, c], f_send.at[t, c], f_recv.at[t, c], row_me, c)

    def relay(t):
        codes = code_recv[t][0:1, :].astype(jnp.int32)
        choose = one_hot(iota((CK, Q), 0) + 1 == codes)
        fwd_buf[t] = mm(choose, chunk_buf[t]).astype(BF16).reshape(C, K, D)
        for d in range(1, C):
            fwd_copy(t, col_of[d]).start()
        rows_buf[t, col_me] = fwd_buf[t, col_me]

    relay(0)

    ones = jnp.ones((SUB, 256), F32)

    squares = []
    for part in range(0, D, 256):
        block = cent_ref[:, part : part + 256].astype(F32)
        squares.append(block * block)
    while len(squares) > 1:
        squares = [a + b for a, b in zip(squares[::2], squares[1::2])] + (
            [squares[-1]] if len(squares) % 2 else []
        )
    cent_sq = lax.dot_general(
        ones, squares[0], (((1,), (1,)), ((), ())), precision=HIGH, preferred_element_type=F32
    )
    cent_inv = lax.rsqrt(cent_sq[0:1, :] + 1.0)

    all_peers(lambda t, r, d: tbl_arrival(t, r, d).wait_recv())

    eye = iota((CK, CK), 0) == iota((CK, CK), 1)

    def spread(t):
        column = jnp.zeros((CK, 1), F32)
        for c in range(C):
            line = tbl_recv[t * C + c][0:1, :]
            here = iota((CK, LANES), 0) - c * K == iota((CK, LANES), 1)
            here = here & (iota((CK, LANES), 1) < K)
            column = column + jnp.sum(jnp.where(here, line, 0.0), axis=1, keepdims=True)
        tag_col[t] = column
        flat = jnp.sum(jnp.where(eye, column, 0.0), axis=0, keepdims=True)
        tag_row[t] = jnp.where(flat > 0.0, flat, -1.0)

    each(0, R, spread)

    stats_ref[...] = jnp.zeros(stats_ref.shape, F32)

    def absorb(t):
        for d in range(1, C):
            fwd_arrival(t, col_of[d]).wait_recv()
        mine = rows_buf[t].reshape(CK, D)
        column = tag_col[t]
        line = tag_row[t]
        gram = mm_t(mine, mine)
        diag = jnp.where(eye, gram, 0.0)
        scale = lax.rsqrt(jnp.sum(diag, axis=1, keepdims=True) + 1.0)
        inv_col[t] = scale
        inv_row[t] = lax.rsqrt(jnp.sum(diag, axis=0, keepdims=True) + 1.0)
        member = iota((CK, S), 1).astype(F32) == column - 1.0
        cross = mm_t(mine, cent_ref[...]) * cent_inv
        similarity = jnp.sum(jnp.where(member, cross, 0.0), axis=1, keepdims=True) * scale
        sim_col[t] = similarity
        stats_ref[0:1, :] += jnp.sum(jnp.where(member, 1.0, 0.0), axis=0, keepdims=True)
        stats_ref[1:2, :] += jnp.sum(jnp.where(member, similarity, 0.0), axis=0, keepdims=True)
        stats_ref[2:3, :] += jnp.sum(
            jnp.where(member, similarity * similarity, 0.0), axis=0, keepdims=True
        )
        same = (column == line) & jnp.logical_not(eye)
        best = jnp.max(jnp.where(same, gram * scale, 0.0), axis=0, keepdims=True)

        def pair(u, best):
            other = rows_buf[u].reshape(CK, D)
            down = mm_t(other, mine)
            up = mm_t(mine, other)
            from_other = jnp.where(tag_col[u] == line, down * inv_col[u], 0.0)
            from_mine = jnp.where(column == tag_row[u], up * scale, 0.0)
            best_row[u] = jnp.maximum(best_row[u], jnp.max(from_mine, axis=0, keepdims=True))
            return jnp.maximum(best, jnp.max(from_other, axis=0, keepdims=True))

        best_row[t] = lax.fori_loop(0, t, pair, best)

    def advance(t, carry):
        code_copy(t, row_of(R - 1)).wait_recv()
        row_copy(t, row_of(R - 1)).wait_recv()
        relay(t)
        absorb(t - 1)
        return carry

    lax.fori_loop(1, R, advance, 0)
    absorb(R - 1)

    floor = jnp.maximum(stats_ref[0:1, :], 1.0)
    mean = stats_ref[1:2, :] / floor
    variance = jnp.maximum(stats_ref[2:3, :] / floor - mean * mean, 0.0)
    out_ref[2:5, :S] = stats_ref[...]
    spread_inv = 1.0 / jnp.sqrt(variance + 1.0 / D)

    def res_copy(t, r, d):
        return remote(
            res_send.at[t * C + col_of[d]],
            res_recv.at[own],
            r_send.at[t * C + d],
            r_recv.at[own],
            r,
            col_of[d],
        )

    def res_arrival(t, r, d):
        o = r * C + col_of[d]
        return remote(
            res_send.at[t * C + col_of[d]], res_recv.at[o], r_send.at[t * C + d], r_recv.at[o], r, col_of[d]
        )

    half = LANES // 2

    def finish(t):
        column = tag_col[t]
        member = iota((CK, S), 1).astype(F32) == column - 1.0
        centre = jnp.sum(jnp.where(member, mean, 0.0), axis=1, keepdims=True)
        width = jnp.sum(jnp.where(member, spread_inv, 0.0), axis=1, keepdims=True)
        proto = (centre - sim_col[t]) * width
        flat = best_row[t] * inv_row[t] * math.sqrt(D)
        redundant = jnp.sum(jnp.where(eye, flat, 0.0), axis=1, keepdims=True)
        lane = iota((CK, LANES), 1)
        rank = lax.rem(iota((CK, LANES), 0), K)
        lined = jnp.where(lane == rank, proto, 0.0) + jnp.where(lane == rank + half, redundant, 0.0)
        gather = lax.shift_right_logical(iota((C * SUB, CK), 0), 3) == lax.div(iota((C * SUB, CK), 1), K)
        packed = lax.dot_general(
            jnp.where(gather, 1.0, 0.0),
            lined,
            (((1,), (0,)), ((), ())),
            precision=HIGH,
            preferred_element_type=F32,
        )
        res_send[pl.ds(t * C, C)] = packed.reshape(C, SUB, LANES)

    def deliver(t):
        finish(t)
        r = row_of(t)
        for d in range(C):
            res_copy(t, r, d).start()

    each(1, R, deliver)
    finish(0)
    for d in range(1, C):
        res_copy(0, row_me, d).start()
    res_recv[own] = res_send[col_me]

    def drain(t):
        code_copy(t, row_of(t)).wait_send()
        row_copy(t, row_of(t)).wait_send()

    each(1, R, drain)

    def drain_fwd(t):
        for d in range(1, C):
            fwd_copy(t, col_of[d]).wait_send()

    each(0, R, drain_fwd)

    def drain_small(t, r, d):
        tbl_copy(t, r, d).wait_send()
        res_copy(t, r, d).wait_send()

    all_peers(drain_small)
    all_peers(lambda t, r, d: res_arrival(t, r, d).wait_recv())

    results = res_recv[...].reshape(O * SUB, LANES).T
    pick_owner = jnp.where(iota((O * SUB, L), 0) == owner_i * SUB, 1.0, 0.0)
    found = lax.dot_general(
        results, pick_owner, (((1,), (0,)), ((), ())), precision=HIGH, preferred_element_type=F32
    )
    sublane = iota((LANES, L), 0)
    out_ref[0:1, :L] = jnp.sum(jnp.where(sublane == rank_i, found, 0.0), axis=0, keepdims=True)
    out_ref[1:2, :L] = jnp.sum(jnp.where(sublane == rank_i + half, found, 0.0), axis=0, keepdims=True)


def local(documents, assigned, centroids, owner_slot):
    L, D = documents.shape
    S = centroids.shape[0]
    R = lax.axis_size("dp")
    C = lax.axis_size("cent")
    O = R * C
    pair_cap = 2 * L // O
    row_cap = 5 * C * pair_cap // 8
    K = round_up(pair_cap, 16)
    Q = round_up(row_cap, 16)
    CK = C * K
    vmem = pl.BlockSpec(memory_space=pltpu.VMEM)
    dma = pltpu.SemaphoreType.DMA
    packed = pl.pallas_call(
        functools.partial(kernel, (R, C, K, Q)),
        name="cluster_exchange",
        out_shape=jax.ShapeDtypeStruct((SUB, max(L, S)), F32),
        in_specs=[vmem] * 4,
        out_specs=vmem,
        scratch_shapes=[
            pltpu.VMEM((R, Q, D), BF16),
            pltpu.VMEM((R, Q, D), BF16),
            pltpu.VMEM((R, SUB, Q), F32),
            pltpu.VMEM((R, SUB, Q), F32),
            pltpu.VMEM((R, C, K, D), BF16),
            pltpu.VMEM((R, C, K, D), BF16),
            pltpu.VMEM((O, SUB, LANES), F32),
            pltpu.VMEM((O, SUB, LANES), F32),
            pltpu.VMEM((O, SUB, LANES), F32),
            pltpu.VMEM((O, SUB, LANES), F32),
            pltpu.VMEM((R, CK, 1), F32),
            pltpu.VMEM((R, 1, CK), F32),
            pltpu.VMEM((R, CK, 1), F32),
            pltpu.VMEM((R, 1, CK), F32),
            pltpu.VMEM((R, CK, 1), F32),
            pltpu.VMEM((R, 1, CK), F32),
            dma((R,)),
            dma((R,)),
            dma((R,)),
            dma((R,)),
            dma((R, C)),
            dma((R, C)),
            dma((O,)),
            dma((O,)),
            dma((O,)),
            dma((O,)),
            pltpu.VMEM((3, S), F32),
        ],
        compiler_params=pltpu.CompilerParams(
            collective_id=0, has_side_effects=True, vmem_limit_bytes=62 * 1024 * 1024
        ),
    )(
        documents,
        assigned.reshape(1, L),
        centroids,
        owner_slot.reshape(-1, LANES),
    )
    return packed[0, :L], packed[1, :L], packed[2:5, :S]


def solution(mesh):
    in_specs = (P(("dp", "cent"), None), P(("dp", "cent")), P(("dp", "cent"), None), P())
    out_specs = (P(("dp", "cent")), P(("dp", "cent")), P(None, ("dp", "cent")))
    return jax.shard_map(local, mesh=mesh, in_specs=in_specs, out_specs=out_specs, check_vma=False)
```

profile of v0, /device:TPU:0, one launch (start us, length us, event | category | flops | bytes accessed | tf_op | source)
XLA Modules:
  0.0 94.3 jit_solution(12000887121356180778)
XLA Ops:
  0.6 90.9 %cluster_exchange.1 = f32[8,512]{1,0:T(8,128)} custom-call(bf16[512,2048]{1,0:T(8,128)(2,1)} %docs_ref.1, s32[1,512]{1,0:T(1,128)} %bitcast.5, bf16[384,2048]{1,0:T(8,128)(2,1)} %cent_ref.1, s32[96,128]{1,0:T(8,128)} %bitcast.4), custom_call_target="tpu_custom_call" | custom-call | tf_op jit(solution)/shard_map/cluster_exchange/pallas_call | solution.py:420
  91.6 1.4 %fusion = (f32[1,512]{1,0:T(1,128)}, f32[1,512]{1,0:T(1,128)}) fusion(f32[8,512]{1,0:T(8,128)} %cluster_exchange.1), kind=kLoop, calls=%fused_computation | loop fusion | bytes 8192 | tf_op jit(solution)/shard_map/slice | solution.py:464
  93.0 1.3 %slice.11 = f32[3,384]{1,0:T(4,128)} slice(f32[8,512]{1,0:T(8,128)} %cluster_exchange.1), slice={[2:5], [0:384]} | slice | bytes 9216 | tf_op jit(solution)/shard_map/slice | solution.py:464
where the time goes:
time: 94.7 us; the launch traced here: 94.3 us
  Pallas kernels  90.9 us (96%)
  local copies, waits for them, and re-layouts  2.68 us (3%)
    pallas_call x1, Pallas kernels, local(): pl.pallas_call(functools.partial(kernel, (R, C, K, Q)), name='cluster_exc...  90.9 us
    slice x2, local copies, waits for them, and re-layouts, local(): return (packed[0, :L], packed[1, :L], packed[2:5, :S])  2.68 us

commit v1 on v0

v1 whole, which is shorter than its diff:
```python
import functools
import math

import jax
import jax.numpy as jnp
from jax import lax
from jax.experimental import pallas as pl
from jax.experimental.pallas import tpu as pltpu
from jax.sharding import PartitionSpec as P

F32 = jnp.float32
BF16 = jnp.bfloat16
LANES = 128
SUB = 8


def round_up(value, unit):
    return -(-value // unit) * unit


def each(low, high, body):
    if high - low <= 8:
        for step in range(low, high):
            body(step)
    else:
        lax.fori_loop(low, high, lambda step, carry: (body(step), carry)[1], 0)


def iota(shape, dim):
    return lax.broadcasted_iota(jnp.int32, shape, dim)


def mm(left, right):
    return lax.dot_general(left, right, (((1,), (0,)), ((), ())), preferred_element_type=F32)


def mm_t(left, right):
    return lax.dot_general(left, right, (((1,), (1,)), ((), ())), preferred_element_type=F32)


def one_hot(condition):
    return jnp.where(condition, 1.0, 0.0).astype(BF16)


def split3(value):
    high = value.astype(BF16)
    rest = value - high.astype(F32)
    mid = rest.astype(BF16)
    low = (rest - mid.astype(F32)).astype(BF16)
    return high, mid, low


def kernel(
    dims,
    docs_hbm,
    assigned_hbm,
    cent_hbm,
    table_hbm,
    out_ref,
    docs_ref,
    assigned_ref,
    table_ref,
    all_buf,
    send_buf,
    chunk_buf,
    code_send,
    code_recv,
    fwd_buf,
    tbl_send,
    tbl_recv,
    res_send,
    res_recv,
    res_rows,
    tag_row,
    tag_mat,
    inv_row,
    inv_mat,
    sim_row,
    best_row,
    best_mat,
    cent_mat,
    gram_acc,
    stats_ref,
    in_sem,
    a_send,
    a_recv,
    m_send,
    m_recv,
    f_send,
    f_recv,
    t_send,
    t_recv,
    r_send,
    r_recv,
):
    R, C, K, Q, PIECES = dims
    O = R * C
    CK = C * K
    L, D = docs_ref.shape
    S = cent_hbm.shape[0]
    T = table_ref.shape[0]
    W = D // PIECES
    QP = code_send.shape[2]
    small = R <= 8
    row_me = lax.axis_index("dp")
    col_me = lax.axis_index("cent")
    own = row_me * C + col_me

    bits = []
    while 2 ** len(bits) < R:
        bits.append(lax.rem(lax.div(row_me, 2 ** len(bits)), 2))
    col_of = [col_me] + [lax.rem(col_me + d, C) for d in range(1, C)]

    def row_of(t):
        total = 0
        for i, bit in enumerate(bits):
            if isinstance(t, int):
                total = total + (1 - bit if (t >> i) & 1 else bit) * 2**i
            else:
                total = total + lax.rem(bit + lax.div(t, 2**i), 2) * 2**i
        return total

    def all_peers(body):
        def at_row(t):
            r = row_of(t)
            for d in range(C):
                body(t, r, d)

        each(1, R, at_row)
        for d in range(1, C):
            body(0, row_me, d)

    def where_is(r, c):
        return {"dp": r, "cent": c}

    def remote(src, dst, send, recv, r, c):
        return pltpu.make_async_remote_copy(
            src_ref=src,
            dst_ref=dst,
            send_sem=send,
            recv_sem=recv,
            device_id=where_is(r, c),
            device_id_type=pl.DeviceIdType.MESH,
        )

    barrier = pltpu.get_barrier_semaphore()

    def greet(t, r, d):
        pl.semaphore_signal(
            barrier, inc=1, device_id=where_is(r, col_of[d]), device_id_type=pl.DeviceIdType.MESH
        )

    all_peers(greet)

    cent_rows = all_buf.at[pl.ds(0, S), :]
    loads = [
        pltpu.make_async_copy(assigned_hbm, assigned_ref, in_sem.at[0]),
        pltpu.make_async_copy(table_hbm, table_ref, in_sem.at[1]),
        pltpu.make_async_copy(docs_hbm, docs_ref, in_sem.at[2]),
        pltpu.make_async_copy(cent_hbm, cent_rows, in_sem.at[3]),
    ]
    for load in loads:
        load.start()
    loads[0].wait()
    loads[1].wait()

    assigned = assigned_ref[...]
    high = lax.shift_right_logical(assigned, 7)
    low = jnp.bitwise_and(assigned, 127)
    table = table_ref[...]
    pick = one_hot(iota((T, L), 0) == high)
    looked = jnp.zeros((LANES, L), F32)
    shift = 0
    while 2**shift < O * S:
        digit = jnp.bitwise_and(lax.shift_right_logical(table, shift), 255)
        looked = looked + float(2**shift) * lax.dot_general(
            digit.astype(F32).astype(BF16), pick, (((0,), (0,)), ((), ())), preferred_element_type=F32
        )
        shift += 8
    slot = jnp.sum(jnp.where(iota((LANES, L), 0) == low, looked, 0.0), axis=0, keepdims=True)
    owner = jnp.floor((slot + 0.5) * (1.0 / S))
    row = jnp.floor((owner + 0.5) * (1.0 / C))
    owner_i = owner.astype(jnp.int32)
    row_i = row.astype(jnp.int32)
    cent_i = owner_i - row_i * C
    is_owner = jnp.where(iota((O, L), 0) == owner_i, 1.0, 0.0)
    is_row = jnp.where(iota((R, L), 0) == row_i, 1.0, 0.0)
    earlier = one_hot(iota((L, L), 0) < iota((L, L), 1))
    ranks = mm(jnp.concatenate([is_owner, is_row], axis=0).astype(BF16), earlier)
    rank_owner = jnp.sum(ranks[:O] * is_owner, axis=0, keepdims=True)
    rank_row = jnp.sum(ranks[O:] * is_row, axis=0, keepdims=True)
    position = jnp.bitwise_xor(row_i, row_me) * Q + rank_row.astype(jnp.int32)
    rank_i = rank_owner.astype(jnp.int32)

    ahead = cent_i - col_me
    ahead = jnp.where(ahead < 0, ahead + C, ahead)
    behind = jnp.where(ahead == 0, 0, C - ahead)
    lane_i = behind * K + rank_i
    code = ((ahead * K + rank_i) + 1).astype(F32).astype(BF16)
    code8 = jnp.broadcast_to(code, (SUB, L))
    is_lane = one_hot(iota((LANES, L), 0) == lane_i)

    tag = slot - owner * S + 1.0
    tag_hi = jnp.floor(tag * (1.0 / 128.0))
    tag_lo = tag - tag_hi * 128.0
    tags = mm_t(jnp.concatenate([is_owner * tag_hi, is_owner * tag_lo], axis=0).astype(BF16), is_lane)
    tags = 128.0 * tags[:O] + tags[O:]
    for o in range(O):
        tbl_send[o] = tags[o : o + 1, :]

    def mark(t):
        line = mm_t(code8, one_hot(iota((QP, L), 0) + t * Q == jnp.where(position < (t + 1) * Q, position, -1)))
        code_send[t] = line[0:1, :]

    each(0, R, mark)

    def row_copy(t, p):
        at = pl.ds(p * W, W)
        return remote(
            send_buf.at[t, :, at], chunk_buf.at[t, :, at], a_send.at[t, p], a_recv.at[t, p], row_of(t), col_me
        )

    def code_copy(t):
        return remote(code_send.at[t], code_recv.at[t], m_send.at[t], m_recv.at[t], row_of(t), col_me)

    def tbl_copy(t, r, d):
        return remote(
            tbl_send.at[r * C + col_of[d]],
            tbl_recv.at[t * C + (C - d) % C],
            t_send.at[t * C + d],
            t_recv.at[t * C + (C - d) % C],
            r,
            col_of[d],
        )

    def tbl_arrival(t, r, d):
        return remote(
            tbl_send.at[r * C + col_of[d]],
            tbl_recv.at[t * C + d],
            t_send.at[t * C + d],
            t_recv.at[t * C + d],
            r,
            col_of[d],
        )

    def start_rows(t):
        for p in range(PIECES):
            row_copy(t, p).start()

    def choose(ts):
        wanted = [one_hot(iota((Q, L), 0) + t * Q == position) for t in ts]
        found = mm(jnp.concatenate(wanted, axis=0), docs_ref[...]).astype(BF16)
        for i, t in enumerate(ts):
            send_buf[t] = found[i * Q : (i + 1) * Q]

    def first_sends():
        pl.semaphore_wait(barrier, O - 1)
        each(1, R, lambda t: code_copy(t).start())
        all_peers(lambda t, r, d: tbl_copy(t, r, d).start())

    loads[2].wait()
    if R == 8:
        inner = lax.rem(bits[-1] + bits[-2], 2) == 1
        far = R // 2
        choose([far, 2])
        first_sends()

        @pl.when(inner)
        def _():
            start_rows(far)

        start_rows(2)
        choose([3, 1])
        start_rows(3)

        @pl.when(jnp.logical_not(inner))
        def _():
            start_rows(far)

        start_rows(1)
        choose([5, 6])
        start_rows(5)
        start_rows(6)
        choose([7, 0])
        start_rows(7)
    else:
        first_sends()
        group = max(1, R // 2)
        for first in range(0, R, group):
            wanted = one_hot(iota((group * Q, L), 0) + first * Q == position)
            send_buf[first : first + group] = (
                mm(wanted, docs_ref[...]).astype(BF16).reshape(group, Q, D)
            )
            each(max(first, 1), first + group, start_rows)
    tbl_recv[0] = tbl_send[own]

    def rows_at(t, block=0, count=None):
        return pl.ds(S + t * CK + block * K, CK if count is None else count)

    def fwd_copy(t, d, p):
        at = pl.ds(p * W, W)
        return remote(
            fwd_buf.at[t, d - 1, :, at],
            all_buf.at[rows_at(t, C - d, K), at],
            f_send.at[t, d, p],
            f_recv.at[t, C - d, p],
            row_me,
            col_of[d],
        )

    def fwd_arrival(t, d, p):
        at = pl.ds(p * W, W)
        return remote(
            fwd_buf.at[t, d - 1, :, at],
            all_buf.at[rows_at(t, d, K), at],
            f_send.at[t, d, p],
            f_recv.at[t, d, p],
            row_me,
            col_of[d],
        )

    def relay(t, p, mine=False):
        if not mine:
            row_copy(t, p).wait_recv()
        at = pl.ds(p * W, W)
        line = (code_send if mine else code_recv)[t][:, :Q].astype(jnp.int32)
        wanted = one_hot(iota((CK, Q), 0) + 1 == line)
        found = mm(wanted, (send_buf if mine else chunk_buf)[t, :, at]).astype(BF16)
        fwd_buf[t, :, :, at] = found[K:].reshape(C - 1, K, W)
        for d in range(1, C):
            fwd_copy(t, d, p).start()
        all_buf[rows_at(t, 0, K), at] = found[:K]

    for p in range(PIECES):
        relay(0, p, True)

    loads[3].wait()
    norm = jnp.zeros((S, LANES), F32)
    for part in range(0, D, LANES):
        block = all_buf[0:S, part : part + LANES].astype(F32)
        norm = norm + block * block
    cent_mat[...] = jnp.broadcast_to(
        lax.rsqrt(jnp.sum(norm, axis=1, keepdims=True) + 1.0), cent_mat.shape
    )

    all_peers(lambda t, r, d: tbl_arrival(t, r, d).wait_recv())

    eye = iota((CK, CK), 0) == iota((CK, CK), 1)

    def spread(t):
        line = tbl_recv[t * C]
        for c in range(1, C):
            line = line + tbl_recv[t * C + c]
        line = line[:, :CK]
        tag_row[t] = line
        tag_mat[t] = jnp.broadcast_to(
            jnp.sum(jnp.where(eye, line, 0.0), axis=1, keepdims=True), (CK, CK)
        )
        best_mat[t] = jnp.zeros((CK, CK), F32)

    each(0, R, spread)
    stats_ref[...] = jnp.zeros(stats_ref.shape, F32)

    def member_of(t):
        return (iota((S, CK), 0) + 1).astype(F32) == tag_row[t]

    def self_block(t, gram):
        diag = jnp.where(eye, gram, 0.0)
        row_scale = lax.rsqrt(jnp.sum(diag, axis=0, keepdims=True) + 1.0)
        col_scale = lax.rsqrt(jnp.sum(diag, axis=1, keepdims=True) + 1.0)
        inv_row[t] = row_scale
        inv_mat[t] = jnp.broadcast_to(col_scale, (CK, CK))
        line = jnp.where(tag_row[t] > 0.0, tag_row[t], -1.0)
        same = (tag_mat[t] == line) & jnp.logical_not(eye)
        best = jnp.max(jnp.where(same, gram * col_scale, 0.0), axis=0, keepdims=True)
        return row_scale, line, best

    def other_block(u, gram, row_scale, line, best):
        same = tag_mat[u] == line
        best_mat[u] = jnp.maximum(best_mat[u], jnp.where(same, gram * row_scale, 0.0))
        return jnp.maximum(
            best, jnp.max(jnp.where(same, gram * inv_mat[u], 0.0), axis=0, keepdims=True)
        )

    def cross_block(t, cross, row_scale):
        member = member_of(t)
        similarity = row_scale * jnp.sum(
            jnp.where(member, cross * cent_mat[...], 0.0), axis=0, keepdims=True
        )
        sim_row[t] = similarity
        lines = [jnp.ones((1, CK), BF16), *split3(similarity), *split3(similarity * similarity)]
        lines = jnp.concatenate(
            [line.astype(F32) for line in lines] + [jnp.zeros((1, CK), F32)], axis=0
        )
        stats_ref[...] += mm_t(lines.astype(BF16), one_hot(member))

    def settle(t, read):
        row_scale, line, best = self_block(t, read(S + t * CK, CK))
        for u in range(t):
            best = other_block(u, read(S + u * CK, CK), row_scale, line, best)
        best_row[t] = best
        cross_block(t, read(0, S), row_scale)

    def arrivals(t, p):
        for d in range(1, C):
            fwd_arrival(t, d, p).wait_recv()

    def absorb(t):
        for p in range(PIECES):
            arrivals(t, p)
        gram_acc[0 : S + (t + 1) * CK] = mm_t(all_buf[0 : S + (t + 1) * CK, :], all_buf[rows_at(t), :])
        settle(t, lambda start, count: gram_acc[start : start + count])

    def absorb_piece(t, p):
        arrivals(t, p)
        at = pl.ds(p * W, W)
        rows = S + (t + 1) * CK
        part = mm_t(all_buf[0:rows, at], all_buf[rows_at(t), at])
        gram_acc[0:rows] = part if p == 0 else gram_acc[0:rows] + part

    def absorb_any(t):
        for p in range(PIECES):
            arrivals(t, p)
        mine = all_buf[rows_at(t), :]
        row_scale, line, best = self_block(t, mm_t(mine, mine))

        def pair(u, best):
            return other_block(u, mm_t(all_buf[rows_at(u), :], mine), row_scale, line, best)

        best_row[t] = lax.fori_loop(0, t, pair, best)
        cross_block(t, mm_t(all_buf[0:S, :], mine), row_scale)

    def relay_all(t):
        code_copy(t).wait_recv()
        for p in range(PIECES):
            relay(t, p)

    if small:
        done = 0
        for t in range(1, R - 1):
            relay_all(t)
            while done < (t + 1 if t == R - 3 else t):
                absorb(done)
                done += 1
        last = R - 1
        code_copy(last).wait_recv()
        half = PIECES // 2
        for p in range(half):
            relay(last, p)
        while done < last:
            absorb(done)
            done += 1
        for p in range(half, PIECES):
            relay(last, p)
            absorb_piece(last, p - half)
        for p in range(PIECES - half, PIECES):
            absorb_piece(last, p)
        settle(last, lambda start, count: gram_acc[start : start + count])
    else:

        def advance(t, carry):
            relay_all(t)
            absorb_any(t - 1)
            return carry

        lax.fori_loop(1, R, advance, 0)
        absorb_any(R - 1)

    stats = stats_ref[...]
    count = stats[0:1]
    total = stats[1:2] + stats[2:3] + stats[3:4]
    square = stats[4:5] + stats[5:6] + stats[6:7]
    floor = jnp.maximum(count, 1.0)
    mean = total / floor
    variance = jnp.maximum(square / floor - mean * mean, 0.0)
    spread_inv = 1.0 / jnp.sqrt(variance + 1.0 / D)
    wanted = [line.astype(F32) for line in (*split3(mean), *split3(spread_inv))]
    wanted = jnp.concatenate(wanted + [jnp.zeros((2, S), F32)], axis=0).astype(BF16)

    def res_copy(t, r, d):
        return remote(
            res_send.at[t], res_recv.at[own], r_send.at[t * C + d], r_recv.at[own], r, col_of[d]
        )

    def res_arrival(t, r, d):
        o = r * C + col_of[d]
        return remote(res_send.at[t], res_recv.at[o], r_send.at[t * C + d], r_recv.at[o], r, col_of[d])

    def finish(t):
        found = mm(wanted, one_hot(member_of(t)))
        centre = found[0:1] + found[1:2] + found[2:3]
        width = found[3:4] + found[4:5] + found[5:6]
        proto = (centre - sim_row[t]) * width
        column = jnp.max(best_mat[t], axis=1, keepdims=True)
        flat = jnp.max(jnp.where(eye, column, 0.0), axis=0, keepdims=True)
        redundant = jnp.maximum(flat, best_row[t]) * inv_row[t] * math.sqrt(D)
        res_send[t, 0:1, :CK] = proto
        res_send[t, 1:2, :CK] = redundant

    if CK < LANES:
        res_send[...] = jnp.zeros(res_send.shape, F32)

    def deliver(t):
        finish(t)
        r = row_of(t)
        for d in range(C):
            res_copy(t, r, d).start()

    if small:
        for t in range(R - 1, 0, -1):
            deliver(t)
    else:
        each(1, R, deliver)
    finish(0)
    for d in range(1, C):
        res_copy(0, row_me, d).start()
    res_recv[own] = res_send[0]
    out_ref[2:3, :S] = count
    out_ref[3:4, :S] = total
    out_ref[4:5, :S] = square

    def drain(t):
        code_copy(t).wait_send()
        for p in range(PIECES):
            row_copy(t, p).wait_send()

    each(1, R, drain)

    def drain_fwd(t):
        for d in range(1, C):
            for p in range(PIECES):
                fwd_copy(t, d, p).wait_send()

    each(0, R, drain_fwd)

    def drain_small(t, r, d):
        tbl_copy(t, r, d).wait_send()
        res_copy(t, r, d).wait_send()

    all_peers(drain_small)
    all_peers(lambda t, r, d: res_arrival(t, r, d).wait_recv())

    for o in range(O):
        pair = res_recv[o]
        res_rows[o : o + 1, :] = pair[0:1]
        res_rows[O + o : O + o + 1, :] = pair[1:2]
    parts = jnp.concatenate([line.astype(F32) for line in split3(res_rows[...])], axis=0)
    found = mm(parts.astype(BF16), is_lane)
    found = found[: 2 * O] + found[2 * O : 4 * O] + found[4 * O :]
    mask = iota((O, L), 0) == owner_i
    out_ref[0:1, :L] = jnp.sum(jnp.where(mask, found[:O], 0.0), axis=0, keepdims=True)
    out_ref[1:2, :L] = jnp.sum(jnp.where(mask, found[O:], 0.0), axis=0, keepdims=True)


def local(documents, assigned, centroids, owner_slot):
    L, D = documents.shape
    S = centroids.shape[0]
    R = lax.axis_size("dp")
    C = lax.axis_size("cent")
    O = R * C
    pair_cap = 2 * L // O
    row_cap = 5 * C * pair_cap // 8
    K = round_up(pair_cap, 16)
    Q = round_up(row_cap, 16)
    CK = C * K
    QP = round_up(Q, LANES)
    pieces = 4 if R <= 8 else 1
    T = owner_slot.shape[0] // LANES
    hbm = pl.BlockSpec(memory_space=pl.ANY)
    dma = pltpu.SemaphoreType.DMA
    packed = pl.pallas_call(
        functools.partial(kernel, (R, C, K, Q, pieces)),
        name="cluster_exchange",
        out_shape=jax.ShapeDtypeStruct((SUB, max(L, S)), F32),
        in_specs=[hbm] * 4,
        out_specs=pl.BlockSpec(memory_space=pltpu.VMEM),
        scratch_shapes=[
            pltpu.VMEM((L, D), BF16),
            pltpu.VMEM((1, L), jnp.int32),
            pltpu.VMEM((T, LANES), jnp.int32),
            pltpu.VMEM((S + R * CK, D), BF16),
            pltpu.VMEM((R, Q, D), BF16),
            pltpu.VMEM((R, Q, D), BF16),
            pltpu.VMEM((R, 1, QP), F32),
            pltpu.VMEM((R, 1, QP), F32),
            pltpu.VMEM((R, C - 1, K, D), BF16),
            pltpu.VMEM((O, 1, LANES), F32),
            pltpu.VMEM((O, 1, LANES), F32),
            pltpu.VMEM((R, 2, LANES), F32),
            pltpu.VMEM((O, 2, LANES), F32),
            pltpu.VMEM((2 * O, LANES), F32),
            pltpu.VMEM((R, 1, CK), F32),
            pltpu.VMEM((R, CK, CK), F32),
            pltpu.VMEM((R, 1, CK), F32),
            pltpu.VMEM((R, CK, CK), F32),
            pltpu.VMEM((R, 1, CK), F32),
            pltpu.VMEM((R, 1, CK), F32),
            pltpu.VMEM((R, CK, CK), F32),
            pltpu.VMEM((S, CK), F32),
            pltpu.VMEM((S + R * CK if R <= 8 else SUB, CK), F32),
            pltpu.VMEM((SUB, S), F32),
            dma((4,)),
            dma((R, pieces)),
            dma((R, pieces)),
            dma((R,)),
            dma((R,)),
            dma((R, C, pieces)),
            dma((R, C, pieces)),
            dma((O,)),
            dma((O,)),
            dma((O,)),
            dma((O,)),
        ],
        compiler_params=pltpu.CompilerParams(
            collective_id=0, has_side_effects=True, vmem_limit_bytes=62 * 1024 * 1024
        ),
    )(
        documents,
        assigned.reshape(1, L),
        centroids,
        owner_slot.reshape(-1, LANES),
    )
    return packed[0, :L], packed[1, :L], packed[2:5, :S]


def solution(mesh):
    in_specs = (P(("dp", "cent"), None), P(("dp", "cent")), P(("dp", "cent"), None), P())
    out_specs = (P(("dp", "cent")), P(("dp", "cent")), P(None, ("dp", "cent")))
    return jax.shard_map(local, mesh=mesh, in_specs=in_specs, out_specs=out_specs, check_vma=False)
```

time: 94.7 us -> 87.9 us (0.928)
  Pallas kernels: 90.9 us -> 84.1 us
    pallas_call x1, Pallas kernels: 90.9 us -> 84.1 us  [local(): pl.pallas_call(functools.partial(kernel, (R, C, K, Q, pieces)), name='clu...]
where the time goes in v1:
time: 87.9 us; the launch traced here: 87.5 us
  Pallas kernels  84.1 us (96%)
  local copies, waits for them, and re-layouts  2.68 us (3%)
    pallas_call x1, Pallas kernels, local(): pl.pallas_call(functools.partial(kernel, (R, C, K, Q, pieces)), name='clu...  84.1 us
    slice x2, local copies, waits for them, and re-layouts, local(): return (packed[0, :L], packed[1, :L], packed[2:5, :S])  2.68 us

profile of v1, /device:TPU:0, one launch (start us, length us, event | category | flops | bytes accessed | tf_op | source)
XLA Modules:
  0.0 87.5 jit_solution(11624731317006658971)
XLA Ops:
  0.6 84.1 %cluster_exchange.1 = f32[8,512]{1,0:T(8,128)} custom-call(bf16[512,2048]{1,0:T(8,128)(2,1)} %docs_hbm.1, s32[1,512]{1,0:T(1,128)} %bitcast.5, bf16[384,2048]{1,0:T(8,128)(2,1)} %cent_hbm.1, s32[96,128]{1,0:T(8,128)} %bitcast.4), custom_call_target="tpu_custom_call" | custom-call | tf_op jit(solution)/shard_map/cluster_exchange/pallas_call | solution.py:571
  84.8 1.4 %fusion = (f32[1,512]{1,0:T(1,128)}, f32[1,512]{1,0:T(1,128)}) fusion(f32[8,512]{1,0:T(8,128)} %cluster_exchange.1), kind=kLoop, calls=%fused_computation | loop fusion | bytes 8192 | tf_op jit(solution)/shard_map/slice | solution.py:623
  86.2 1.3 %slice.11 = f32[3,384]{1,0:T(4,128)} slice(f32[8,512]{1,0:T(8,128)} %cluster_exchange.1), slice={[2:5], [0:384]} | slice | bytes 9216 | tf_op jit(solution)/shard_map/slice | solution.py:623

commit v2 on v1

--- a/solution.py
+++ b/solution.py
@@ -217,31 +217,27 @@
     def row_copy(t, p):
         at = pl.ds(p * W, W)
         return remote(
-            send_buf.at[t, :, at], chunk_buf.at[t, :, at], a_send.at[t, p], a_recv.at[t, p], row_of(t), col_me
+            send_buf.at[t, :, at], chunk_buf.at[t, :, at], a_send.at[0], a_recv.at[t, p], row_of(t), col_me
         )
 
     def code_copy(t):
-        return remote(code_send.at[t], code_recv.at[t], m_send.at[t], m_recv.at[t], row_of(t), col_me)
+        return remote(code_send.at[t], code_recv.at[t], m_send.at[0], m_recv.at[0], row_of(t), col_me)
 
     def tbl_copy(t, r, d):
         return remote(
             tbl_send.at[r * C + col_of[d]],
             tbl_recv.at[t * C + (C - d) % C],
-            t_send.at[t * C + d],
-            t_recv.at[t * C + (C - d) % C],
+            t_send.at[0],
+            t_recv.at[0],
             r,
             col_of[d],
         )
 
-    def tbl_arrival(t, r, d):
-        return remote(
-            tbl_send.at[r * C + col_of[d]],
-            tbl_recv.at[t * C + d],
-            t_send.at[t * C + d],
-            t_recv.at[t * C + d],
-            r,
-            col_of[d],
-        )
+    def whole(ref, send, recv):
+        return remote(ref, ref, send.at[0], recv.at[0], row_of(1), col_me)
+
+    tbl_all = whole(tbl_recv.at[pl.ds(1, O - 1)], t_send, t_recv)
+    code_all = whole(code_recv.at[pl.ds(1, R - 1)], m_send, m_recv)
 
     def start_rows(t):
         for p in range(PIECES):
@@ -302,22 +298,15 @@
         return remote(
             fwd_buf.at[t, d - 1, :, at],
             all_buf.at[rows_at(t, C - d, K), at],
-            f_send.at[t, d, p],
-            f_recv.at[t, C - d, p],
+            f_send.at[0],
+            f_recv.at[t, p],
             row_me,
             col_of[d],
         )
 
-    def fwd_arrival(t, d, p):
-        at = pl.ds(p * W, W)
-        return remote(
-            fwd_buf.at[t, d - 1, :, at],
-            all_buf.at[rows_at(t, d, K), at],
-            f_send.at[t, d, p],
-            f_recv.at[t, d, p],
-            row_me,
-            col_of[d],
-        )
+    def fwd_arrival(t, p):
+        ref = all_buf.at[rows_at(t, 1, CK - K), pl.ds(p * W, W)]
+        return remote(ref, ref, f_send.at[0], f_recv.at[t, p], row_me, col_of[1])
 
     def relay(t, p, mine=False):
         if not mine:
@@ -343,7 +332,8 @@
         lax.rsqrt(jnp.sum(norm, axis=1, keepdims=True) + 1.0), cent_mat.shape
     )
 
-    all_peers(lambda t, r, d: tbl_arrival(t, r, d).wait_recv())
+    tbl_all.wait_recv()
+    code_all.wait_recv()
 
     eye = iota((CK, CK), 0) == iota((CK, CK), 1)
 
@@ -402,14 +392,7 @@
         cross_block(t, read(0, S), row_scale)
 
     def arrivals(t, p):
-        for d in range(1, C):
-            fwd_arrival(t, d, p).wait_recv()
-
-    def absorb(t):
-        for p in range(PIECES):
-            arrivals(t, p)
-        gram_acc[0 : S + (t + 1) * CK] = mm_t(all_buf[0 : S + (t + 1) * CK, :], all_buf[rows_at(t), :])
-        settle(t, lambda start, count: gram_acc[start : start + count])
+        fwd_arrival(t, p).wait_recv()
 
     def absorb_piece(t, p):
         arrivals(t, p)
@@ -417,6 +400,12 @@
         rows = S + (t + 1) * CK
         part = mm_t(all_buf[0:rows, at], all_buf[rows_at(t), at])
         gram_acc[0:rows] = part if p == 0 else gram_acc[0:rows] + part
+        if p == PIECES - 1:
+            settle(t, lambda start, count: gram_acc[start : start + count])
+
+    def absorb(t):
+        for p in range(PIECES):
+            absorb_piece(t, p)
 
     def absorb_any(t):
         for p in range(PIECES):
@@ -431,31 +420,23 @@
         cross_block(t, mm_t(all_buf[0:S, :], mine), row_scale)
 
     def relay_all(t):
-        code_copy(t).wait_recv()
         for p in range(PIECES):
             relay(t, p)
 
     if small:
         done = 0
-        for t in range(1, R - 1):
+        for t in range(1, R - 2):
             relay_all(t)
             while done < (t + 1 if t == R - 3 else t):
                 absorb(done)
                 done += 1
-        last = R - 1
-        code_copy(last).wait_recv()
-        half = PIECES // 2
-        for p in range(half):
-            relay(last, p)
-        while done < last:
-            absorb(done)
-            done += 1
-        for p in range(half, PIECES):
-            relay(last, p)
-            absorb_piece(last, p - half)
-        for p in range(PIECES - half, PIECES):
-            absorb_piece(last, p)
-        settle(last, lambda start, count: gram_acc[start : start + count])
+        steps = [(t, p) for t in (R - 2, R - 1) for p in range(PIECES)]
+        lag = 2
+        for i in range(len(steps) + lag):
+            if i < len(steps):
+                relay(*steps[i])
+            if i >= lag:
+                absorb_piece(*steps[i - lag])
     else:
 
         def advance(t, carry):
@@ -479,15 +460,12 @@
 
     def res_copy(t, r, d):
         return remote(
-            res_send.at[t], res_recv.at[own], r_send.at[t * C + d], r_recv.at[own], r, col_of[d]
-        )
-
-    def res_arrival(t, r, d):
-        o = r * C + col_of[d]
-        return remote(res_send.at[t], res_recv.at[o], r_send.at[t * C + d], r_recv.at[o], r, col_of[d])
-
-    def finish(t):
-        found = mm(wanted, one_hot(member_of(t)))
+            res_send.at[t], res_recv.at[t * C + (C - d) % C], r_send.at[0], r_recv.at[0], r, col_of[d]
+        )
+
+    res_all = whole(res_recv.at[pl.ds(1, O - 1)], r_send, r_recv)
+
+    def finish(t, found):
         centre = found[0:1] + found[1:2] + found[2:3]
         width = found[3:4] + found[4:5] + found[5:6]
         proto = (centre - sim_row[t]) * width
@@ -501,44 +479,39 @@
         res_send[...] = jnp.zeros(res_send.shape, F32)
 
     def deliver(t):
-        finish(t)
         r = row_of(t)
-        for d in range(C):
-            res_copy(t, r, d).start()
+        for d in (2, 3, 1, 0) if C == 4 else range(C):
+            if not (isinstance(t, int) and t == 0 and d == 0):
+                res_copy(t, r, d).start()
 
     if small:
-        for t in range(R - 1, 0, -1):
+        members = jnp.concatenate([one_hot(member_of(t)) for t in range(R)], axis=1)
+        found = mm(wanted, members)
+        for t in range(R):
+            finish(t, found[:, t * CK : (t + 1) * CK])
+        for t in [5, 4, 7, 6, 3, 2, 1, 0] if R == 8 else range(R):
             deliver(t)
     else:
+
+        def finish_any(t):
+            finish(t, mm(wanted, one_hot(member_of(t))))
+
+        each(0, R, finish_any)
         each(1, R, deliver)
-    finish(0)
-    for d in range(1, C):
-        res_copy(0, row_me, d).start()
-    res_recv[own] = res_send[0]
+        deliver(0)
+    res_recv[0] = res_send[0]
     out_ref[2:3, :S] = count
     out_ref[3:4, :S] = total
     out_ref[4:5, :S] = square
 
-    def drain(t):
-        code_copy(t).wait_send()
-        for p in range(PIECES):
-            row_copy(t, p).wait_send()
-
-    each(1, R, drain)
-
-    def drain_fwd(t):
-        for d in range(1, C):
-            for p in range(PIECES):
-                fwd_copy(t, d, p).wait_send()
-
-    each(0, R, drain_fwd)
-
-    def drain_small(t, r, d):
-        tbl_copy(t, r, d).wait_send()
-        res_copy(t, r, d).wait_send()
-
-    all_peers(drain_small)
-    all_peers(lambda t, r, d: res_arrival(t, r, d).wait_recv())
+    remote(
+        send_buf.at[pl.ds(1, R - 1)], send_buf.at[pl.ds(1, R - 1)], a_send.at[0], a_recv.at[0, 0], row_of(1), col_me
+    ).wait_send()
+    code_all.wait_send()
+    tbl_all.wait_send()
+    remote(fwd_buf, fwd_buf, f_send.at[0], f_recv.at[0, 0], row_me, col_of[1]).wait_send()
+    res_all.wait_send()
+    res_all.wait_recv()
 
     for o in range(O):
         pair = res_recv[o]
@@ -547,7 +520,7 @@
     parts = jnp.concatenate([line.astype(F32) for line in split3(res_rows[...])], axis=0)
     found = mm(parts.astype(BF16), is_lane)
     found = found[: 2 * O] + found[2 * O : 4 * O] + found[4 * O :]
-    mask = iota((O, L), 0) == owner_i
+    mask = iota((O, L), 0) == jnp.bitwise_xor(row_i, row_me) * C + ahead
     out_ref[0:1, :L] = jnp.sum(jnp.where(mask, found[:O], 0.0), axis=0, keepdims=True)
     out_ref[1:2, :L] = jnp.sum(jnp.where(mask, found[O:], 0.0), axis=0, keepdims=True)
 
@@ -600,16 +573,16 @@
             pltpu.VMEM((S + R * CK if R <= 8 else SUB, CK), F32),
             pltpu.VMEM((SUB, S), F32),
             dma((4,)),
+            dma((1,)),
             dma((R, pieces)),
+            dma((1,)),
+            dma((1,)),
+            dma((1,)),
             dma((R, pieces)),
-            dma((R,)),
-            dma((R,)),
-            dma((R, C, pieces)),
-            dma((R, C, pieces)),
-            dma((O,)),
-            dma((O,)),
-            dma((O,)),
-            dma((O,)),
+            dma((1,)),
+            dma((1,)),
+            dma((1,)),
+            dma((1,)),
         ],
         compiler_params=pltpu.CompilerParams(
             collective_id=0, has_side_effects=True, vmem_limit_bytes=62 * 1024 * 1024

time: 87.9 us -> 81.1 us (0.923)
  Pallas kernels: 84.1 us -> 77.4 us
    pallas_call x1, Pallas kernels: 84.1 us -> 77.4 us  [local(): pl.pallas_call(functools.partial(kernel, (R, C, K, Q, pieces)), name='clu...]
where the time goes in v2:
time: 81.1 us; the launch traced here: 80.7 us
  Pallas kernels  77.4 us (95%)
  local copies, waits for them, and re-layouts  2.68 us (3%)
    pallas_call x1, Pallas kernels, local(): pl.pallas_call(functools.partial(kernel, (R, C, K, Q, pieces)), name='clu...  77.4 us
    slice x2, local copies, waits for them, and re-layouts, local(): return (packed[0, :L], packed[1, :L], packed[2:5, :S])  2.68 us

profile of v2, /device:TPU:0, one launch (start us, length us, event | category | flops | bytes accessed | tf_op | source)
XLA Modules:
  0.0 80.7 jit_solution(4044774200669734011)
XLA Ops:
  0.6 77.4 %cluster_exchange.1 = f32[8,512]{1,0:T(8,128)} custom-call(bf16[512,2048]{1,0:T(8,128)(2,1)} %docs_hbm.1, s32[1,512]{1,0:T(1,128)} %bitcast.5, bf16[384,2048]{1,0:T(8,128)(2,1)} %cent_hbm.1, s32[96,128]{1,0:T(8,128)} %bitcast.4), custom_call_target="tpu_custom_call" | custom-call | tf_op jit(solution)/shard_map/cluster_exchange/pallas_call | solution.py:544
  78.0 1.4 %fusion = (f32[1,512]{1,0:T(1,128)}, f32[1,512]{1,0:T(1,128)}) fusion(f32[8,512]{1,0:T(8,128)} %cluster_exchange.1), kind=kLoop, calls=%fused_computation | loop fusion | bytes 8192 | tf_op jit(solution)/shard_map/slice | solution.py:596
  79.4 1.3 %slice.11 = f32[3,384]{1,0:T(4,128)} slice(f32[8,512]{1,0:T(8,128)} %cluster_exchange.1), slice={[2:5], [0:384]} | slice | bytes 9216 | tf_op jit(solution)/shard_map/slice | solution.py:596

commit v3 on v2

--- a/solution.py
+++ b/solution.py
@@ -66,8 +66,8 @@
     code_send,
     code_recv,
     fwd_buf,
-    tbl_send,
-    tbl_recv,
+    tag_send,
+    tag_recv,
     res_send,
     res_recv,
     res_rows,
@@ -93,13 +93,12 @@
     r_send,
     r_recv,
 ):
-    R, C, K, Q, PIECES = dims
+    R, C, K, Q, cuts = dims
     O = R * C
     CK = C * K
     L, D = docs_ref.shape
     S = cent_hbm.shape[0]
     T = table_ref.shape[0]
-    W = D // PIECES
     QP = code_send.shape[2]
     small = R <= 8
     row_me = lax.axis_index("dp")
@@ -111,8 +110,12 @@
         bits.append(lax.rem(lax.div(row_me, 2 ** len(bits)), 2))
     col_of = [col_me] + [lax.rem(col_me + d, C) for d in range(1, C)]
 
+    swap = {3: 4, 4: 3} if R == 8 else {}
+
     def row_of(t):
         total = 0
+        if isinstance(t, int):
+            t = swap.get(t, t)
         for i, bit in enumerate(bits):
             if isinstance(t, int):
                 total = total + (1 - bit if (t >> i) & 1 else bit) * 2**i
@@ -145,12 +148,14 @@
 
     barrier = pltpu.get_barrier_semaphore()
 
-    def greet(t, r, d):
+    def greet(r, c):
         pl.semaphore_signal(
-            barrier, inc=1, device_id=where_is(r, col_of[d]), device_id_type=pl.DeviceIdType.MESH
-        )
-
-    all_peers(greet)
+            barrier, inc=1, device_id=where_is(r, c), device_id_type=pl.DeviceIdType.MESH
+        )
+
+    each(1, R, lambda t: greet(row_of(t), col_me))
+    for d in range(1, C):
+        greet(row_me, col_of[d])
 
     cent_rows = all_buf.at[pl.ds(0, S), :]
     loads = [
@@ -189,58 +194,59 @@
     ranks = mm(jnp.concatenate([is_owner, is_row], axis=0).astype(BF16), earlier)
     rank_owner = jnp.sum(ranks[:O] * is_owner, axis=0, keepdims=True)
     rank_row = jnp.sum(ranks[O:] * is_row, axis=0, keepdims=True)
-    position = jnp.bitwise_xor(row_i, row_me) * Q + rank_row.astype(jnp.int32)
+    block_i = jnp.bitwise_xor(row_i, row_me)
+    if swap:
+        block_i = jnp.where((block_i == 3) | (block_i == 4), 7 - block_i, block_i)
+    position = block_i * Q + rank_row.astype(jnp.int32)
     rank_i = rank_owner.astype(jnp.int32)
 
     ahead = cent_i - col_me
     ahead = jnp.where(ahead < 0, ahead + C, ahead)
     behind = jnp.where(ahead == 0, 0, C - ahead)
     lane_i = behind * K + rank_i
-    code = ((ahead * K + rank_i) + 1).astype(F32).astype(BF16)
-    code8 = jnp.broadcast_to(code, (SUB, L))
     is_lane = one_hot(iota((LANES, L), 0) == lane_i)
 
     tag = slot - owner * S + 1.0
     tag_hi = jnp.floor(tag * (1.0 / 128.0))
-    tag_lo = tag - tag_hi * 128.0
-    tags = mm_t(jnp.concatenate([is_owner * tag_hi, is_owner * tag_lo], axis=0).astype(BF16), is_lane)
-    tags = 128.0 * tags[:O] + tags[O:]
-    for o in range(O):
-        tbl_send[o] = tags[o : o + 1, :]
+    lines = jnp.concatenate(
+        [(ahead * K + rank_i + 1).astype(F32), tag_hi, tag - tag_hi * 128.0, jnp.zeros((SUB - 3, L), F32)],
+        axis=0,
+    ).astype(BF16)
 
     def mark(t):
-        line = mm_t(code8, one_hot(iota((QP, L), 0) + t * Q == jnp.where(position < (t + 1) * Q, position, -1)))
-        code_send[t] = line[0:1, :]
+        here = jnp.where(position < (t + 1) * Q, position, -1)
+        line = mm_t(lines, one_hot(iota((QP, L), 0) + t * Q == here))
+        code_send[t, 0:1, :] = line[0:1]
+        code_send[t, 1:2, :] = 128.0 * line[1:2] + line[2:3]
 
     each(0, R, mark)
 
+    def cut(t, p):
+        width = cuts[t][p] if small else D
+        return pl.ds(sum(cuts[t][:p]) if small else 0, width), width
+
+    def sem(t, p):
+        return sum(len(c) for c in cuts[:t]) + p if small else t
+
+    def pieces(t):
+        return range(len(cuts[t])) if small else range(1)
+
     def row_copy(t, p):
-        at = pl.ds(p * W, W)
+        at = cut(t, p)[0]
         return remote(
-            send_buf.at[t, :, at], chunk_buf.at[t, :, at], a_send.at[0], a_recv.at[t, p], row_of(t), col_me
+            send_buf.at[t, :, at], chunk_buf.at[t, :, at], a_send.at[0], a_recv.at[sem(t, p)], row_of(t), col_me
         )
 
     def code_copy(t):
         return remote(code_send.at[t], code_recv.at[t], m_send.at[0], m_recv.at[0], row_of(t), col_me)
 
-    def tbl_copy(t, r, d):
-        return remote(
-            tbl_send.at[r * C + col_of[d]],
-            tbl_recv.at[t * C + (C - d) % C],
-            t_send.at[0],
-            t_recv.at[0],
-            r,
-            col_of[d],
-        )
-
     def whole(ref, send, recv):
         return remote(ref, ref, send.at[0], recv.at[0], row_of(1), col_me)
 
-    tbl_all = whole(tbl_recv.at[pl.ds(1, O - 1)], t_send, t_recv)
     code_all = whole(code_recv.at[pl.ds(1, R - 1)], m_send, m_recv)
 
     def start_rows(t):
-        for p in range(PIECES):
+        for p in pieces(t):
             row_copy(t, p).start()
 
     def choose(ts):
@@ -250,30 +256,28 @@
             send_buf[t] = found[i * Q : (i + 1) * Q]
 
     def first_sends():
-        pl.semaphore_wait(barrier, O - 1)
+        pl.semaphore_wait(barrier, R + C - 2)
         each(1, R, lambda t: code_copy(t).start())
-        all_peers(lambda t, r, d: tbl_copy(t, r, d).start())
 
     loads[2].wait()
     if R == 8:
         inner = lax.rem(bits[-1] + bits[-2], 2) == 1
-        far = R // 2
-        choose([far, 2])
+        choose([3, 1])
         first_sends()
 
         @pl.when(inner)
         def _():
-            start_rows(far)
-
+            start_rows(3)
+
+        start_rows(1)
+        choose([2, 4])
         start_rows(2)
-        choose([3, 1])
-        start_rows(3)
+        start_rows(4)
 
         @pl.when(jnp.logical_not(inner))
         def _():
-            start_rows(far)
-
-        start_rows(1)
+            start_rows(3)
+
         choose([5, 6])
         start_rows(5)
         start_rows(6)
@@ -288,40 +292,62 @@
                 mm(wanted, docs_ref[...]).astype(BF16).reshape(group, Q, D)
             )
             each(max(first, 1), first + group, start_rows)
-    tbl_recv[0] = tbl_send[own]
 
     def rows_at(t, block=0, count=None):
         return pl.ds(S + t * CK + block * K, CK if count is None else count)
 
     def fwd_copy(t, d, p):
-        at = pl.ds(p * W, W)
+        at = cut(t, p)[0]
         return remote(
             fwd_buf.at[t, d - 1, :, at],
             all_buf.at[rows_at(t, C - d, K), at],
             f_send.at[0],
-            f_recv.at[t, p],
+            f_recv.at[sem(t, p)],
             row_me,
             col_of[d],
         )
 
     def fwd_arrival(t, p):
-        ref = all_buf.at[rows_at(t, 1, CK - K), pl.ds(p * W, W)]
-        return remote(ref, ref, f_send.at[0], f_recv.at[t, p], row_me, col_of[1])
+        ref = all_buf.at[rows_at(t, 1, CK - K), cut(t, p)[0]]
+        return remote(ref, ref, f_send.at[0], f_recv.at[sem(t, p)], row_me, col_of[1])
+
+    def tag_copy(t, d):
+        return remote(
+            tag_send.at[t], tag_recv.at[t, C - d], t_send.at[0], t_recv.at[t], row_me, col_of[d]
+        )
+
+    def tag_arrival(t):
+        ref = tag_recv.at[t, pl.ds(1, C - 1)]
+        return remote(ref, ref, t_send.at[0], t_recv.at[t], row_me, col_of[1])
+
+    block = iota((CK, Q), 0) // K
+    turned = jnp.where(block == 0, 0, C - block) * K + iota((CK, Q), 0) - block * K + 1
 
     def relay(t, p, mine=False):
         if not mine:
             row_copy(t, p).wait_recv()
-        at = pl.ds(p * W, W)
-        line = (code_send if mine else code_recv)[t][:, :Q].astype(jnp.int32)
+        at, width = cut(t, p)
+        lines = (code_send if mine else code_recv)[t][:, :Q]
+        line = lines[0:1].astype(jnp.int32)
         wanted = one_hot(iota((CK, Q), 0) + 1 == line)
+        if p == 0:
+            high = jnp.floor(lines[1:2] * (1.0 / 128.0))
+            digits = [high, lines[1:2] - high * 128.0, jnp.zeros((SUB - 2, Q), F32)]
+            digits = mm_t(jnp.concatenate(digits, axis=0).astype(BF16), one_hot(turned == line))
+            tag_send[t, 0:1, :CK] = 128.0 * digits[0:1] + digits[1:2]
+            for d in range(1, C):
+                tag_copy(t, d).start()
         found = mm(wanted, (send_buf if mine else chunk_buf)[t, :, at]).astype(BF16)
-        fwd_buf[t, :, :, at] = found[K:].reshape(C - 1, K, W)
+        fwd_buf[t, :, :, at] = found[K:].reshape(C - 1, K, width)
         for d in range(1, C):
             fwd_copy(t, d, p).start()
         all_buf[rows_at(t, 0, K), at] = found[:K]
 
-    for p in range(PIECES):
+    if CK < LANES:
+        tag_send[...] = jnp.zeros(tag_send.shape, F32)
+    for p in pieces(0):
         relay(0, p, True)
+    code_all.wait_recv()
 
     loads[3].wait()
     norm = jnp.zeros((S, LANES), F32)
@@ -332,23 +358,20 @@
         lax.rsqrt(jnp.sum(norm, axis=1, keepdims=True) + 1.0), cent_mat.shape
     )
 
-    tbl_all.wait_recv()
-    code_all.wait_recv()
 
     eye = iota((CK, CK), 0) == iota((CK, CK), 1)
 
     def spread(t):
-        line = tbl_recv[t * C]
+        tag_arrival(t).wait_recv()
+        line = tag_send[t][:, :CK]
         for c in range(1, C):
-            line = line + tbl_recv[t * C + c]
-        line = line[:, :CK]
+            line = jnp.where(iota((1, CK), 1) // K == c, tag_recv[t, c][:, :CK], line)
         tag_row[t] = line
         tag_mat[t] = jnp.broadcast_to(
             jnp.sum(jnp.where(eye, line, 0.0), axis=1, keepdims=True), (CK, CK)
         )
         best_mat[t] = jnp.zeros((CK, CK), F32)
 
-    each(0, R, spread)
     stats_ref[...] = jnp.zeros(stats_ref.shape, F32)
 
     def member_of(t):
@@ -395,21 +418,23 @@
         fwd_arrival(t, p).wait_recv()
 
     def absorb_piece(t, p):
+        if p == 0:
+            spread(t)
         arrivals(t, p)
-        at = pl.ds(p * W, W)
+        at = cut(t, p)[0]
         rows = S + (t + 1) * CK
         part = mm_t(all_buf[0:rows, at], all_buf[rows_at(t), at])
         gram_acc[0:rows] = part if p == 0 else gram_acc[0:rows] + part
-        if p == PIECES - 1:
+        if p == len(cuts[t]) - 1:
             settle(t, lambda start, count: gram_acc[start : start + count])
 
     def absorb(t):
-        for p in range(PIECES):
+        for p in pieces(t):
             absorb_piece(t, p)
 
     def absorb_any(t):
-        for p in range(PIECES):
-            arrivals(t, p)
+        spread(t)
+        arrivals(t, 0)
         mine = all_buf[rows_at(t), :]
         row_scale, line, best = self_block(t, mm_t(mine, mine))
 
@@ -419,24 +444,36 @@
         best_row[t] = lax.fori_loop(0, t, pair, best)
         cross_block(t, mm_t(all_buf[0:S, :], mine), row_scale)
 
-    def relay_all(t):
-        for p in range(PIECES):
-            relay(t, p)
-
-    if small:
-        done = 0
-        for t in range(1, R - 2):
+    def relay_all(*ts):
+        for p in pieces(ts[0]):
+            for t in ts:
+                relay(t, p)
+
+    if R == 8:
+        relay_all(1)
+        absorb(0)
+        relay_all(2, 3)
+        absorb(1)
+        relay(4, 0)
+        relay(5, 0)
+        absorb(2)
+        relay(4, 1)
+        relay(5, 1)
+        absorb(3)
+        absorb(4)
+        absorb(5)
+        steps = [(t, p) for t in (6, 7) for p in pieces(t)]
+        lag = 3
+        for i in range(-lag, len(steps)):
+            if i + lag < len(steps):
+                relay(*steps[i + lag])
+            if i >= 0:
+                absorb_piece(*steps[i])
+    elif small:
+        for t in range(1, R):
             relay_all(t)
-            while done < (t + 1 if t == R - 3 else t):
-                absorb(done)
-                done += 1
-        steps = [(t, p) for t in (R - 2, R - 1) for p in range(PIECES)]
-        lag = 2
-        for i in range(len(steps) + lag):
-            if i < len(steps):
-                relay(*steps[i])
-            if i >= lag:
-                absorb_piece(*steps[i - lag])
+            absorb(t - 1)
+        absorb(R - 1)
     else:
 
         def advance(t, carry):
@@ -489,7 +526,7 @@
         found = mm(wanted, members)
         for t in range(R):
             finish(t, found[:, t * CK : (t + 1) * CK])
-        for t in [5, 4, 7, 6, 3, 2, 1, 0] if R == 8 else range(R):
+        for t in [5, 3, 7, 6, 4, 2, 1, 0] if R == 8 else range(R):
             deliver(t)
     else:
 
@@ -505,11 +542,12 @@
     out_ref[4:5, :S] = square
 
     remote(
-        send_buf.at[pl.ds(1, R - 1)], send_buf.at[pl.ds(1, R - 1)], a_send.at[0], a_recv.at[0, 0], row_of(1), col_me
+        send_buf.at[pl.ds(1, R - 1)], send_buf.at[pl.ds(1, R - 1)], a_send.at[0], a_recv.at[0], row_of(1), col_me
     ).wait_send()
     code_all.wait_send()
-    tbl_all.wait_send()
-    remote(fwd_buf, fwd_buf, f_send.at[0], f_recv.at[0, 0], row_me, col_of[1]).wait_send()
+    ref = tag_recv.at[:, pl.ds(1, C - 1)]
+    remote(ref, ref, t_send.at[0], t_recv.at[0], row_me, col_of[1]).wait_send()
+    remote(fwd_buf, fwd_buf, f_send.at[0], f_recv.at[0], row_me, col_of[1]).wait_send()
     res_all.wait_send()
     res_all.wait_recv()
 
@@ -520,7 +558,7 @@
     parts = jnp.concatenate([line.astype(F32) for line in split3(res_rows[...])], axis=0)
     found = mm(parts.astype(BF16), is_lane)
     found = found[: 2 * O] + found[2 * O : 4 * O] + found[4 * O :]
-    mask = iota((O, L), 0) == jnp.bitwise_xor(row_i, row_me) * C + ahead
+    mask = iota((O, L), 0) == block_i * C + ahead
     out_ref[0:1, :L] = jnp.sum(jnp.where(mask, found[:O], 0.0), axis=0, keepdims=True)
     out_ref[1:2, :L] = jnp.sum(jnp.where(mask, found[O:], 0.0), axis=0, keepdims=True)
 
@@ -537,14 +575,16 @@
     Q = round_up(row_cap, 16)
     CK = C * K
     QP = round_up(Q, LANES)
-    pieces = 4 if R <= 8 else 1
+    half, unit = D // 2, D // 8
+    cuts = [(half, half)] * (R - 2) + [(2 * unit,) * 4, (2 * unit,) * 3 + (unit,) * 2]
+    copies = sum(len(c) for c in cuts) if R <= 8 else R
     T = owner_slot.shape[0] // LANES
     hbm = pl.BlockSpec(memory_space=pl.ANY)
     dma = pltpu.SemaphoreType.DMA
     packed = pl.pallas_call(
-        functools.partial(kernel, (R, C, K, Q, pieces)),
+        functools.partial(kernel, (R, C, K, Q, cuts)),
         name="cluster_exchange",
-        out_shape=jax.ShapeDtypeStruct((SUB, max(L, S)), F32),
+        out_shape=pltpu.VMEM((SUB, max(L, S)), F32),
         in_specs=[hbm] * 4,
         out_specs=pl.BlockSpec(memory_space=pltpu.VMEM),
         scratch_shapes=[
@@ -554,11 +594,11 @@
             pltpu.VMEM((S + R * CK, D), BF16),
             pltpu.VMEM((R, Q, D), BF16),
             pltpu.VMEM((R, Q, D), BF16),
-            pltpu.VMEM((R, 1, QP), F32),
-            pltpu.VMEM((R, 1, QP), F32),
+            pltpu.VMEM((R, 2, QP), F32),
+            pltpu.VMEM((R, 2, QP), F32),
             pltpu.VMEM((R, C - 1, K, D), BF16),
-            pltpu.VMEM((O, 1, LANES), F32),
-            pltpu.VMEM((O, 1, LANES), F32),
+            pltpu.VMEM((R, 1, LANES), F32),
+            pltpu.VMEM((R, C, 1, LANES), F32),
             pltpu.VMEM((R, 2, LANES), F32),
             pltpu.VMEM((O, 2, LANES), F32),
             pltpu.VMEM((2 * O, LANES), F32),
@@ -574,13 +614,13 @@
             pltpu.VMEM((SUB, S), F32),
             dma((4,)),
             dma((1,)),
-            dma((R, pieces)),
+            dma((copies,)),
             dma((1,)),
             dma((1,)),
             dma((1,)),
-            dma((R, pieces)),
+            dma((copies,)),
             dma((1,)),
-            dma((1,)),
+            dma((R,)),
             dma((1,)),
             dma((1,)),
         ],

time: 81.1 us -> 76.1 us (0.938)
  Pallas kernels: 77.4 us -> 74.2 us
  local copies, waits for them, and re-layouts: 2.68 us -> 1.18 us
    pallas_call x1, Pallas kernels: 77.4 us -> 74.2 us  [local(): pl.pallas_call(functools.partial(kernel, (R, C, K, Q, cuts)), name='clust...]
    slice x2, local copies, waits for them, and re-layouts: 2.68 us -> 1.18 us  [local(): return (packed[0, :L], packed[1, :L], packed[2:5, :S])]
where the time goes in v3:
time: 76.1 us; the launch traced here: 76 us
  Pallas kernels  74.2 us (98%)
  local copies, waits for them, and re-layouts  1.18 us (2%)
    pallas_call x1, Pallas kernels, local(): pl.pallas_call(functools.partial(kernel, (R, C, K, Q, cuts)), name='clust...  74.2 us

profile of v3, /device:TPU:0, one launch (start us, length us, event | category | flops | bytes accessed | tf_op | source)
XLA Modules:
  0.0 76.0 jit_solution(8491998290605677672)
XLA Ops:
  0.6 74.2 %cluster_exchange.1 = f32[8,512]{1,0:T(8,128)S(1)} custom-call(bf16[512,2048]{1,0:T(8,128)(2,1)} %docs_hbm.1, s32[1,512]{1,0:T(1,128)} %bitcast.5, bf16[384,2048]{1,0:T(8,128)(2,1)} %cent_hbm.1, s32[96,128]{1,0:T(8,128)} %bitcast.4), custom_call_target="tpu_custom_call" | custom-call | tf_op jit(solution)/shard_map/cluster_exchange/pallas_call | solution.py:584
  74.8 0.6 fusion
  75.4 0.6 slice.11

commit v4 on v3

--- a/solution.py
+++ b/solution.py
@@ -66,6 +66,7 @@
     code_send,
     code_recv,
     fwd_buf,
+    dir_buf,
     tag_send,
     tag_recv,
     res_send,
@@ -92,6 +93,7 @@
     t_recv,
     r_send,
     r_recv,
+    d_send,
 ):
     R, C, K, Q, cuts = dims
     O = R * C
@@ -101,6 +103,7 @@
     T = table_ref.shape[0]
     QP = code_send.shape[2]
     small = R <= 8
+    direct = R == 8
     row_me = lax.axis_index("dp")
     col_me = lax.axis_index("cent")
     own = row_me * C + col_me
@@ -231,23 +234,39 @@
     def pieces(t):
         return range(len(cuts[t])) if small else range(1)
 
+    def ends(t, p):
+        return int(direct and t == R - 1 and p == len(cuts[t]) - 1)
+
     def row_copy(t, p):
         at = cut(t, p)[0]
         return remote(
-            send_buf.at[t, :, at], chunk_buf.at[t, :, at], a_send.at[0], a_recv.at[sem(t, p)], row_of(t), col_me
+            send_buf.at[t, :, at], chunk_buf.at[t, :, at], a_send.at[ends(t, p)], a_recv.at[sem(t, p)], row_of(t), col_me
         )
 
     def code_copy(t):
-        return remote(code_send.at[t], code_recv.at[t], m_send.at[0], m_recv.at[0], row_of(t), col_me)
+        return remote(code_send.at[t], code_recv.at[t], m_send.at[0], m_recv.at[t], row_of(t), col_me)
 
     def whole(ref, send, recv):
         return remote(ref, ref, send.at[0], recv.at[0], row_of(1), col_me)
 
-    code_all = whole(code_recv.at[pl.ds(1, R - 1)], m_send, m_recv)
 
     def start_rows(t):
         for p in pieces(t):
-            row_copy(t, p).start()
+            if not ends(t, p):
+                row_copy(t, p).start()
+
+    def rows_at(t, block=0, count=None):
+        return pl.ds(S + t * CK + block * K, CK if count is None else count)
+
+    def dir_copy(d):
+        return remote(
+            dir_buf.at[d],
+            all_buf.at[rows_at(7, (C - d) % C, K), cut(7, len(cuts[7]) - 1)[0]],
+            d_send.at[0],
+            f_recv.at[sem(7, len(cuts[7]) - 1)],
+            row_of(7),
+            col_of[d],
+        )
 
     def choose(ts):
         wanted = [one_hot(iota((Q, L), 0) + t * Q == position) for t in ts]
@@ -283,6 +302,17 @@
         start_rows(6)
         choose([7, 0])
         start_rows(7)
+        final = len(cuts[7]) - 1
+
+        @pl.when(inner)
+        def _():
+            wanted = one_hot(iota((CK, L), 0) == jnp.where(block_i == 7, ahead * K + rank_i, -1))
+            found = mm(wanted, docs_ref[:, D - cuts[7][final] :]).astype(BF16)
+            dir_buf[...] = found.reshape(dir_buf.shape)
+
+        @pl.when(jnp.logical_not(inner))
+        def _():
+            row_copy(7, final).start()
     else:
         first_sends()
         group = max(1, R // 2)
@@ -293,15 +323,12 @@
             )
             each(max(first, 1), first + group, start_rows)
 
-    def rows_at(t, block=0, count=None):
-        return pl.ds(S + t * CK + block * K, CK if count is None else count)
-
     def fwd_copy(t, d, p):
         at = cut(t, p)[0]
         return remote(
             fwd_buf.at[t, d - 1, :, at],
             all_buf.at[rows_at(t, C - d, K), at],
-            f_send.at[0],
+            f_send.at[ends(t, p)],
             f_recv.at[sem(t, p)],
             row_me,
             col_of[d],
@@ -311,6 +338,10 @@
         ref = all_buf.at[rows_at(t, 1, CK - K), cut(t, p)[0]]
         return remote(ref, ref, f_send.at[0], f_recv.at[sem(t, p)], row_me, col_of[1])
 
+    def dir_arrival(t, p):
+        ref = all_buf.at[rows_at(t), cut(t, p)[0]]
+        return remote(ref, ref, d_send.at[0], f_recv.at[sem(t, p)], row_me, col_of[1])
+
     def tag_copy(t, d):
         return remote(
             tag_send.at[t], tag_recv.at[t, C - d], t_send.at[0], t_recv.at[t], row_me, col_of[d]
@@ -324,7 +355,17 @@
     turned = jnp.where(block == 0, 0, C - block) * K + iota((CK, Q), 0) - block * K + 1
 
     def relay(t, p, mine=False):
+        if ends(t, p):
+            pl.when(jnp.logical_not(inner))(lambda: relay_now(t, p))
+        else:
+            relay_now(t, p, mine)
+
+    def relay_now(t, p, mine=False):
         if not mine:
+            if p == 0 and direct and t == R - 1:
+                pl.when(jnp.logical_not(inner))(lambda: code_copy(t).wait_recv())
+            elif p == 0:
+                code_copy(t).wait_recv()
             row_copy(t, p).wait_recv()
         at, width = cut(t, p)
         lines = (code_send if mine else code_recv)[t][:, :Q]
@@ -347,7 +388,6 @@
         tag_send[...] = jnp.zeros(tag_send.shape, F32)
     for p in pieces(0):
         relay(0, p, True)
-    code_all.wait_recv()
 
     loads[3].wait()
     norm = jnp.zeros((S, LANES), F32)
@@ -415,7 +455,18 @@
         cross_block(t, read(0, S), row_scale)
 
     def arrivals(t, p):
-        fwd_arrival(t, p).wait_recv()
+        if ends(t, p):
+
+            @pl.when(inner)
+            def _():
+                dir_arrival(t, p).wait_recv()
+
+            @pl.when(jnp.logical_not(inner))
+            def _():
+                fwd_arrival(t, p).wait_recv()
+
+        else:
+            fwd_arrival(t, p).wait_recv()
 
     def absorb_piece(t, p):
         if p == 0:
@@ -423,10 +474,40 @@
         arrivals(t, p)
         at = cut(t, p)[0]
         rows = S + (t + 1) * CK
+        before = gram_acc[0:rows] if p else None
         part = mm_t(all_buf[0:rows, at], all_buf[rows_at(t), at])
-        gram_acc[0:rows] = part if p == 0 else gram_acc[0:rows] + part
+        gram_acc[0:rows] = part if p == 0 else before + part
         if p == len(cuts[t]) - 1:
             settle(t, lambda start, count: gram_acc[start : start + count])
+
+    def absorb_last():
+        t = R - 1
+        n = len(cuts[t])
+        width = cuts[t][0]
+        rows = S + R * CK
+        spread(t)
+
+        def step(p, carry):
+            at = pl.ds(pl.multiple_of(p * width, width), width)
+            semaphore = f_recv.at[sem(t, 0) + p]
+            straight = jnp.logical_and(inner, p == n - 1)
+
+            @pl.when(straight)
+            def _():
+                ref = all_buf.at[rows_at(t), at]
+                remote(ref, ref, d_send.at[0], semaphore, row_me, col_of[1]).wait_recv()
+
+            @pl.when(jnp.logical_not(straight))
+            def _():
+                ref = all_buf.at[rows_at(t, 1, CK - K), at]
+                remote(ref, ref, d_send.at[0], semaphore, row_me, col_of[1]).wait_recv()
+
+            before = jnp.where(p > 0, gram_acc[0:rows], 0.0)
+            gram_acc[0:rows] = before + mm_t(all_buf[0:rows, at], all_buf[rows_at(t), at])
+            return carry
+
+        lax.fori_loop(0, n, step, 0)
+        settle(t, lambda start, count: gram_acc[start : start + count])
 
     def absorb(t):
         for p in pieces(t):
@@ -451,6 +532,13 @@
 
     if R == 8:
         relay_all(1)
+
+        @pl.when(inner)
+        def _():
+            code_copy(7).wait_recv()
+            for d in range(C):
+                dir_copy(d).start()
+
         absorb(0)
         relay_all(2, 3)
         absorb(1)
@@ -464,11 +552,13 @@
         absorb(5)
         steps = [(t, p) for t in (6, 7) for p in pieces(t)]
         lag = 3
-        for i in range(-lag, len(steps)):
-            if i + lag < len(steps):
-                relay(*steps[i + lag])
+        for i in range(-lag, len(cuts[6])):
+            relay(*steps[i + lag])
             if i >= 0:
                 absorb_piece(*steps[i])
+        for step in steps[len(cuts[6]) + lag :]:
+            relay(*step)
+        absorb_last()
     elif small:
         for t in range(1, R):
             relay_all(t)
@@ -541,13 +631,30 @@
     out_ref[3:4, :S] = total
     out_ref[4:5, :S] = square
 
-    remote(
-        send_buf.at[pl.ds(1, R - 1)], send_buf.at[pl.ds(1, R - 1)], a_send.at[0], a_recv.at[0], row_of(1), col_me
-    ).wait_send()
-    code_all.wait_send()
-    ref = tag_recv.at[:, pl.ds(1, C - 1)]
-    remote(ref, ref, t_send.at[0], t_recv.at[0], row_me, col_of[1]).wait_send()
-    remote(fwd_buf, fwd_buf, f_send.at[0], f_recv.at[0], row_me, col_of[1]).wait_send()
+    def sent(ref, semaphore):
+        remote(ref, ref, semaphore, r_recv.at[0], row_me, col_of[1]).wait_send()
+
+    if direct:
+        kept = D - cuts[-1][-1]
+        sent(send_buf.at[pl.ds(1, R - 2)], a_send.at[0])
+        sent(send_buf.at[R - 1, :, pl.ds(0, kept)], a_send.at[0])
+        sent(fwd_buf.at[pl.ds(0, R - 1)], f_send.at[0])
+        sent(fwd_buf.at[R - 1, :, :, pl.ds(0, kept)], f_send.at[0])
+
+        @pl.when(inner)
+        def _():
+            sent(dir_buf, d_send.at[0])
+
+        @pl.when(jnp.logical_not(inner))
+        def _():
+            sent(send_buf.at[R - 1, :, pl.ds(kept, D - kept)], a_send.at[1])
+            sent(fwd_buf.at[R - 1, :, :, pl.ds(kept, D - kept)], f_send.at[1])
+
+    else:
+        sent(send_buf.at[pl.ds(1, R - 1)], a_send.at[0])
+        sent(fwd_buf, f_send.at[0])
+    sent(code_recv.at[pl.ds(1, R - 1)], m_send.at[0])
+    sent(tag_recv.at[:, pl.ds(1, C - 1)], t_send.at[0])
     res_all.wait_send()
     res_all.wait_recv()
 
@@ -576,7 +683,7 @@
     CK = C * K
     QP = round_up(Q, LANES)
     half, unit = D // 2, D // 8
-    cuts = [(half, half)] * (R - 2) + [(2 * unit,) * 4, (2 * unit,) * 3 + (unit,) * 2]
+    cuts = [(half, half)] * (R - 2) + [(2 * unit,) * 4] * 2
     copies = sum(len(c) for c in cuts) if R <= 8 else R
     T = owner_slot.shape[0] // LANES
     hbm = pl.BlockSpec(memory_space=pl.ANY)
@@ -597,6 +704,7 @@
             pltpu.VMEM((R, 2, QP), F32),
             pltpu.VMEM((R, 2, QP), F32),
             pltpu.VMEM((R, C - 1, K, D), BF16),
+            pltpu.VMEM((C, K, cuts[-1][-1]), BF16),
             pltpu.VMEM((R, 1, LANES), F32),
             pltpu.VMEM((R, C, 1, LANES), F32),
             pltpu.VMEM((R, 2, LANES), F32),
@@ -613,14 +721,15 @@
             pltpu.VMEM((S + R * CK if R <= 8 else SUB, CK), F32),
             pltpu.VMEM((SUB, S), F32),
             dma((4,)),
-            dma((1,)),
-            dma((copies,)),
-            dma((1,)),
-            dma((1,)),
-            dma((1,)),
+            dma((2,)),
             dma((copies,)),
             dma((1,)),
             dma((R,)),
+            dma((2,)),
+            dma((copies,)),
+            dma((1,)),
+            dma((R,)),
+            dma((1,)),
             dma((1,)),
             dma((1,)),
         ],

time: 76.1 us -> 74.7 us (0.982)
  Pallas kernels: 74.2 us -> 72.7 us
    pallas_call x1, Pallas kernels: 74.2 us -> 72.7 us  [local(): pl.pallas_call(functools.partial(kernel, (R, C, K, Q, cuts)), name='clust...]
where the time goes in v4:
time: 74.7 us; the launch traced here: 74.5 us
  Pallas kernels  72.7 us (97%)
  local copies, waits for them, and re-layouts  1.18 us (2%)
    pallas_call x1, Pallas kernels, local(): pl.pallas_call(functools.partial(kernel, (R, C, K, Q, cuts)), name='clust...  72.7 us

profile of v4, /device:TPU:0, one launch (start us, length us, event | category | flops | bytes accessed | tf_op | source)
XLA Modules:
  0.0 74.5 jit_solution(4618162135278524655)
XLA Ops:
  0.6 72.7 %cluster_exchange.1 = f32[8,512]{1,0:T(8,128)S(1)} custom-call(bf16[512,2048]{1,0:T(8,128)(2,1)} %docs_hbm.1, s32[1,512]{1,0:T(1,128)} %bitcast.5, bf16[384,2048]{1,0:T(8,128)(2,1)} %cent_hbm.1, s32[96,128]{1,0:T(8,128)} %bitcast.4), custom_call_target="tpu_custom_call" | custom-call | tf_op jit(solution)/shard_map/cluster_exchange/pallas_call | solution.py:691
  73.3 0.6 fusion
  73.9 0.6 slice.11

commit v5 on v4

--- a/solution.py
+++ b/solution.py
@@ -95,7 +95,8 @@
     r_recv,
     d_send,
 ):
-    R, C, K, Q, cuts = dims
+    R, C, K, Q, cuts, straight = dims
+    tail = straight * cuts[-1][-1]
     O = R * C
     CK = C * K
     L, D = docs_ref.shape
@@ -112,6 +113,8 @@
     while 2 ** len(bits) < R:
         bits.append(lax.rem(lax.div(row_me, 2 ** len(bits)), 2))
     col_of = [col_me] + [lax.rem(col_me + d, C) for d in range(1, C)]
+
+    plan = [0, 1, 2, 3, -1, 100, 101, -2, 102, 103, -3, 104, -4]
 
     swap = {3: 4, 4: 3} if R == 8 else {}
 
@@ -235,12 +238,12 @@
         return range(len(cuts[t])) if small else range(1)
 
     def ends(t, p):
-        return int(direct and t == R - 1 and p == len(cuts[t]) - 1)
+        return int(direct and t == R - 1 and p >= len(cuts[t]) - straight)
 
     def row_copy(t, p):
         at = cut(t, p)[0]
         return remote(
-            send_buf.at[t, :, at], chunk_buf.at[t, :, at], a_send.at[ends(t, p)], a_recv.at[sem(t, p)], row_of(t), col_me
+            send_buf.at[t, :, at], chunk_buf.at[t, :, at], a_send.at[ends(t, p)], a_recv.at[sem(t, p) - 1], row_of(t), col_me
         )
 
     def code_copy(t):
@@ -261,9 +264,9 @@
     def dir_copy(d):
         return remote(
             dir_buf.at[d],
-            all_buf.at[rows_at(7, (C - d) % C, K), cut(7, len(cuts[7]) - 1)[0]],
+            all_buf.at[rows_at(7, (C - d) % C, K), pl.ds(D - tail, tail)],
             d_send.at[0],
-            f_recv.at[sem(7, len(cuts[7]) - 1)],
+            f_recv.at[sem(7, len(cuts[7]) - straight)],
             row_of(7),
             col_of[d],
         )
@@ -302,17 +305,18 @@
         start_rows(6)
         choose([7, 0])
         start_rows(7)
-        final = len(cuts[7]) - 1
+        final = len(cuts[7]) - straight
 
         @pl.when(inner)
         def _():
             wanted = one_hot(iota((CK, L), 0) == jnp.where(block_i == 7, ahead * K + rank_i, -1))
-            found = mm(wanted, docs_ref[:, D - cuts[7][final] :]).astype(BF16)
+            found = mm(wanted, docs_ref[:, D - tail :]).astype(BF16)
             dir_buf[...] = found.reshape(dir_buf.shape)
 
         @pl.when(jnp.logical_not(inner))
         def _():
-            row_copy(7, final).start()
+            for p in range(final, len(cuts[7])):
+                row_copy(7, p).start()
     else:
         first_sends()
         group = max(1, R // 2)
@@ -337,10 +341,6 @@
     def fwd_arrival(t, p):
         ref = all_buf.at[rows_at(t, 1, CK - K), cut(t, p)[0]]
         return remote(ref, ref, f_send.at[0], f_recv.at[sem(t, p)], row_me, col_of[1])
-
-    def dir_arrival(t, p):
-        ref = all_buf.at[rows_at(t), cut(t, p)[0]]
-        return remote(ref, ref, d_send.at[0], f_recv.at[sem(t, p)], row_me, col_of[1])
 
     def tag_copy(t, d):
         return remote(
@@ -455,18 +455,7 @@
         cross_block(t, read(0, S), row_scale)
 
     def arrivals(t, p):
-        if ends(t, p):
-
-            @pl.when(inner)
-            def _():
-                dir_arrival(t, p).wait_recv()
-
-            @pl.when(jnp.logical_not(inner))
-            def _():
-                fwd_arrival(t, p).wait_recv()
-
-        else:
-            fwd_arrival(t, p).wait_recv()
+        fwd_arrival(t, p).wait_recv()
 
     def absorb_piece(t, p):
         if p == 0:
@@ -487,17 +476,18 @@
         rows = S + R * CK
         spread(t)
 
-        def step(p, carry):
+        slow = n - straight - 1
+
+        def step(i, carry):
+            p = jnp.where(i < slow, i, jnp.where(i < n - 1, i + 1, slow))
             at = pl.ds(pl.multiple_of(p * width, width), width)
             semaphore = f_recv.at[sem(t, 0) + p]
-            straight = jnp.logical_and(inner, p == n - 1)
-
-            @pl.when(straight)
+            @pl.when(jnp.logical_and(inner, p == n - straight))
             def _():
-                ref = all_buf.at[rows_at(t), at]
+                ref = all_buf.at[rows_at(t), pl.ds(D - tail, tail)]
                 remote(ref, ref, d_send.at[0], semaphore, row_me, col_of[1]).wait_recv()
 
-            @pl.when(jnp.logical_not(straight))
+            @pl.when(jnp.logical_or(jnp.logical_not(inner), p < n - straight))
             def _():
                 ref = all_buf.at[rows_at(t, 1, CK - K), at]
                 remote(ref, ref, d_send.at[0], semaphore, row_me, col_of[1]).wait_recv()
@@ -550,14 +540,13 @@
         absorb(3)
         absorb(4)
         absorb(5)
-        steps = [(t, p) for t in (6, 7) for p in pieces(t)]
-        lag = 3
-        for i in range(-lag, len(cuts[6])):
-            relay(*steps[i + lag])
-            if i >= 0:
-                absorb_piece(*steps[i])
-        for step in steps[len(cuts[6]) + lag :]:
-            relay(*step)
+        for step in plan:
+            if step < 0:
+                absorb_piece(6, -1 - step)
+            else:
+                relay(6 + step // 100, step % 100)
+        for p in range(len(cuts[7]) - straight, len(cuts[7])):
+            relay(7, p)
         absorb_last()
     elif small:
         for t in range(1, R):
@@ -635,7 +624,7 @@
         remote(ref, ref, semaphore, r_recv.at[0], row_me, col_of[1]).wait_send()
 
     if direct:
-        kept = D - cuts[-1][-1]
+        kept = D - tail
         sent(send_buf.at[pl.ds(1, R - 2)], a_send.at[0])
         sent(send_buf.at[R - 1, :, pl.ds(0, kept)], a_send.at[0])
         sent(fwd_buf.at[pl.ds(0, R - 1)], f_send.at[0])
@@ -683,13 +672,14 @@
     CK = C * K
     QP = round_up(Q, LANES)
     half, unit = D // 2, D // 8
-    cuts = [(half, half)] * (R - 2) + [(2 * unit,) * 4] * 2
+    cuts = [(D,)] + [(half, half)] * (R - 3) + [(2 * unit,) * 4, (unit,) * 8]
+    straight = 3
     copies = sum(len(c) for c in cuts) if R <= 8 else R
     T = owner_slot.shape[0] // LANES
     hbm = pl.BlockSpec(memory_space=pl.ANY)
     dma = pltpu.SemaphoreType.DMA
     packed = pl.pallas_call(
-        functools.partial(kernel, (R, C, K, Q, cuts)),
+        functools.partial(kernel, (R, C, K, Q, cuts, straight)),
         name="cluster_exchange",
         out_shape=pltpu.VMEM((SUB, max(L, S)), F32),
         in_specs=[hbm] * 4,
@@ -704,7 +694,7 @@
             pltpu.VMEM((R, 2, QP), F32),
             pltpu.VMEM((R, 2, QP), F32),
             pltpu.VMEM((R, C - 1, K, D), BF16),
-            pltpu.VMEM((C, K, cuts[-1][-1]), BF16),
+            pltpu.VMEM((C, K, straight * cuts[-1][-1]), BF16),
             pltpu.VMEM((R, 1, LANES), F32),
             pltpu.VMEM((R, C, 1, LANES), F32),
             pltpu.VMEM((R, 2, LANES), F32),
@@ -722,7 +712,7 @@
             pltpu.VMEM((SUB, S), F32),
             dma((4,)),
             dma((2,)),
-            dma((copies,)),
+            dma((copies - 1,)),
             dma((1,)),
             dma((R,)),
             dma((2,)),
@@ -742,7 +732,27 @@
         centroids,
         owner_slot.reshape(-1, LANES),
     )
-    return packed[0, :L], packed[1, :L], packed[2:5, :S]
+
+    def spill(packed_ref, proto_ref, red_ref, stats_ref, sems):
+        copies = [
+            pltpu.make_async_copy(packed_ref.at[pl.ds(0, 1), pl.ds(0, L)], proto_ref, sems.at[0]),
+            pltpu.make_async_copy(packed_ref.at[pl.ds(1, 1), pl.ds(0, L)], red_ref, sems.at[1]),
+            pltpu.make_async_copy(packed_ref.at[pl.ds(2, 3), pl.ds(0, S)], stats_ref, sems.at[2]),
+        ]
+        for copy in copies:
+            copy.start()
+        for copy in copies:
+            copy.wait()
+
+    proto, red, stats = pl.pallas_call(
+        spill,
+        name="spill",
+        out_shape=[jax.ShapeDtypeStruct((1, L), F32)] * 2 + [jax.ShapeDtypeStruct((3, S), F32)],
+        in_specs=[pl.BlockSpec(memory_space=pltpu.VMEM)],
+        out_specs=[hbm] * 3,
+        scratch_shapes=[dma((3,))],
+    )(pltpu.with_memory_space_constraint(packed, pltpu.VMEM))
+    return proto.reshape(L), red.reshape(L), stats
 
 
 def solution(mesh):

time: 74.7 us -> 74 us (level)
  local copies, waits for them, and re-layouts: 1.18 us -> 0 us
    slice x2 -> x0, local copies, waits for them, and re-layouts: 1.18 us -> none  [local(): return (packed[0, :L], packed[1, :L], packed[2:5, :S])]
    pallas_call x1 -> x2, Pallas kernels: 72.7 us -> 73 us  [the longest x1 72.4 us: local(): pl.pallas_call(functools.partial(kernel, (R, C, K, Q, cuts, straight)), n...]
where the time goes in v5:
time: 74 us; the launch traced here: 73.8 us
  Pallas kernels  73 us (99%)
  between operations  0.8 us (1%)
    pallas_call x1, Pallas kernels, local(): pl.pallas_call(functools.partial(kernel, (R, C, K, Q, cuts, straight)), n...  72.4 us

profile of v5, /device:TPU:0, one launch (start us, length us, event | category | flops | bytes accessed | tf_op | source)
XLA Modules:
  0.0 73.8 jit_solution(8692315089775209774)
XLA Ops:
  0.6 72.4 %cluster_exchange.1.packed_ref = f32[8,512]{1,0:T(8,128)S(1)} custom-call(bf16[512,2048]{1,0:T(8,128)(2,1)} %docs_hbm.1, s32[1,512]{1,0:T(1,128)} %bitcast.5, bf16[384,2048]{1,0:T(8,128)(2,1)} %cent_hbm.1, s32[96,128]{1,0:T(8,128)} %bitcast.4), custom_call_target="tpu_custom_call" | custom-call | tf_op jit(solution)/shard_map/cluster_exchange/pallas_call | solution.py:681
  73.0 0.6 spill.1

commit v6 on v5

--- a/solution.py
+++ b/solution.py
@@ -114,8 +114,6 @@
         bits.append(lax.rem(lax.div(row_me, 2 ** len(bits)), 2))
     col_of = [col_me] + [lax.rem(col_me + d, C) for d in range(1, C)]
 
-    plan = [0, 1, 2, 3, -1, 100, 101, -2, 102, 103, -3, 104, -4]
-
     swap = {3: 4, 4: 3} if R == 8 else {}
 
     def row_of(t):
@@ -246,8 +244,11 @@
             send_buf.at[t, :, at], chunk_buf.at[t, :, at], a_send.at[ends(t, p)], a_recv.at[sem(t, p) - 1], row_of(t), col_me
         )
 
+    def code_group(t):
+        return (0 if t == 1 else 2 if t == R - 1 else 1) if direct else t
+
     def code_copy(t):
-        return remote(code_send.at[t], code_recv.at[t], m_send.at[0], m_recv.at[t], row_of(t), col_me)
+        return remote(code_send.at[t], code_recv.at[t], m_send.at[0], m_recv.at[code_group(t)], row_of(t), col_me)
 
     def whole(ref, send, recv):
         return remote(ref, ref, send.at[0], recv.at[0], row_of(1), col_me)
@@ -261,12 +262,13 @@
     def rows_at(t, block=0, count=None):
         return pl.ds(S + t * CK + block * K, CK if count is None else count)
 
-    def dir_copy(d):
+    def dir_copy(d, p):
+        at, width = cut(7, p)
         return remote(
-            dir_buf.at[d],
-            all_buf.at[rows_at(7, (C - d) % C, K), pl.ds(D - tail, tail)],
+            dir_buf.at[d, :, pl.ds((p - len(cuts[7]) + straight) * width, width)],
+            all_buf.at[rows_at(7, (C - d) % C, K), at],
             d_send.at[0],
-            f_recv.at[sem(7, len(cuts[7]) - straight)],
+            f_recv.at[sem(7, p)],
             row_of(7),
             col_of[d],
         )
@@ -364,7 +366,7 @@
         if not mine:
             if p == 0 and direct and t == R - 1:
                 pl.when(jnp.logical_not(inner))(lambda: code_copy(t).wait_recv())
-            elif p == 0:
+            elif p == 0 and not (direct and 1 < t < R - 1):
                 code_copy(t).wait_recv()
             row_copy(t, p).wait_recv()
         at, width = cut(t, p)
@@ -469,30 +471,37 @@
         if p == len(cuts[t]) - 1:
             settle(t, lambda start, count: gram_acc[start : start + count])
 
-    def absorb_last():
-        t = R - 1
+    def absorb_loop(t):
         n = len(cuts[t])
         width = cuts[t][0]
-        rows = S + R * CK
+        rows = S + (t + 1) * CK
+        first_straight = n - straight if t == R - 1 else n
+        slow = first_straight - 1
         spread(t)
 
-        slow = n - straight - 1
-
         def step(i, carry):
-            p = jnp.where(i < slow, i, jnp.where(i < n - 1, i + 1, slow))
+            p = i
+            if first_straight < n:
+                ahead_of = jnp.logical_and(i >= slow, i < n - 2)
+                p = jnp.where(i == n - 2, slow, i + jnp.where(ahead_of, 1, 0))
             at = pl.ds(pl.multiple_of(p * width, width), width)
             semaphore = f_recv.at[sem(t, 0) + p]
-            @pl.when(jnp.logical_and(inner, p == n - straight))
-            def _():
-                ref = all_buf.at[rows_at(t), pl.ds(D - tail, tail)]
-                remote(ref, ref, d_send.at[0], semaphore, row_me, col_of[1]).wait_recv()
-
-            @pl.when(jnp.logical_or(jnp.logical_not(inner), p < n - straight))
-            def _():
+
+            def relayed():
                 ref = all_buf.at[rows_at(t, 1, CK - K), at]
                 remote(ref, ref, d_send.at[0], semaphore, row_me, col_of[1]).wait_recv()
 
-            before = jnp.where(p > 0, gram_acc[0:rows], 0.0)
+            if first_straight < n:
+
+                @pl.when(jnp.logical_and(inner, p >= first_straight))
+                def _():
+                    ref = all_buf.at[rows_at(t), at]
+                    remote(ref, ref, d_send.at[0], semaphore, row_me, col_of[1]).wait_recv()
+
+                pl.when(jnp.logical_or(jnp.logical_not(inner), p < first_straight))(relayed)
+            else:
+                relayed()
+            before = jnp.where(i > 0, gram_acc[0:rows], 0.0)
             gram_acc[0:rows] = before + mm_t(all_buf[0:rows, at], all_buf[rows_at(t), at])
             return carry
 
@@ -526,11 +535,22 @@
         @pl.when(inner)
         def _():
             code_copy(7).wait_recv()
-            for d in range(C):
-                dir_copy(d).start()
+            for p in range(len(cuts[7]) - straight, len(cuts[7])):
+                for d in range(C):
+                    dir_copy(d, p).start()
 
         absorb(0)
-        relay_all(2, 3)
+        ref = code_recv.at[pl.ds(2, R - 3)]
+        remote(ref, ref, m_send.at[0], m_recv.at[1], row_of(1), col_me).wait_recv()
+
+        @pl.when(inner)
+        def _():
+            relay_all(2, 3)
+
+        @pl.when(jnp.logical_not(inner))
+        def _():
+            relay_all(3, 2)
+
         absorb(1)
         relay(4, 0)
         relay(5, 0)
@@ -540,14 +560,10 @@
         absorb(3)
         absorb(4)
         absorb(5)
-        for step in plan:
-            if step < 0:
-                absorb_piece(6, -1 - step)
-            else:
-                relay(6 + step // 100, step % 100)
-        for p in range(len(cuts[7]) - straight, len(cuts[7])):
-            relay(7, p)
-        absorb_last()
+        relay_all(6)
+        relay_all(7)
+        absorb_loop(6)
+        absorb_loop(R - 1)
     elif small:
         for t in range(1, R):
             relay_all(t)
@@ -567,10 +583,10 @@
     count = stats[0:1]
     total = stats[1:2] + stats[2:3] + stats[3:4]
     square = stats[4:5] + stats[5:6] + stats[6:7]
-    floor = jnp.maximum(count, 1.0)
-    mean = total / floor
-    variance = jnp.maximum(square / floor - mean * mean, 0.0)
-    spread_inv = 1.0 / jnp.sqrt(variance + 1.0 / D)
+    share = 1.0 / jnp.maximum(count, 1.0)
+    mean = total * share
+    variance = jnp.maximum(square * share - mean * mean, 0.0)
+    spread_inv = lax.rsqrt(variance + 1.0 / D)
     wanted = [line.astype(F32) for line in (*split3(mean), *split3(spread_inv))]
     wanted = jnp.concatenate(wanted + [jnp.zeros((2, S), F32)], axis=0).astype(BF16)
 
@@ -672,8 +688,8 @@
     CK = C * K
     QP = round_up(Q, LANES)
     half, unit = D // 2, D // 8
-    cuts = [(D,)] + [(half, half)] * (R - 3) + [(2 * unit,) * 4, (unit,) * 8]
-    straight = 3
+    cuts = [(D,)] + [(half, half)] * (R - 3) + [(2 * unit,) * 4, (2 * unit,) * 4]
+    straight = 2
     copies = sum(len(c) for c in cuts) if R <= 8 else R
     T = owner_slot.shape[0] // LANES
     hbm = pl.BlockSpec(memory_space=pl.ANY)
@@ -714,7 +730,7 @@
             dma((2,)),
             dma((copies - 1,)),
             dma((1,)),
-            dma((R,)),
+            dma((3 if R == 8 else R,)),
             dma((2,)),
             dma((copies,)),
             dma((1,)),

time: 74 us -> 73.4 us (level)
  no operation moved by 1% of the time
where the time goes in v6:
time: 73.4 us; the launch traced here: 73.2 us
  Pallas kernels  72.6 us (99%)
    pallas_call x1, Pallas kernels, local(): pl.pallas_call(functools.partial(kernel, (R, C, K, Q, cuts, straight)), n...  72 us

profile of v6, /device:TPU:0, one launch (start us, length us, event | category | flops | bytes accessed | tf_op | source)
XLA Modules:
  0.0 73.2 jit_solution(16788768153149840923)
XLA Ops:
  0.6 72.0 %cluster_exchange.1.packed_ref = f32[8,512]{1,0:T(8,128)S(1)} custom-call(bf16[512,2048]{1,0:T(8,128)(2,1)} %docs_hbm.1, s32[1,512]{1,0:T(1,128)} %bitcast.5, bf16[384,2048]{1,0:T(8,128)(2,1)} %cent_hbm.1, s32[96,128]{1,0:T(8,128)} %bitcast.4), custom_call_target="tpu_custom_call" | custom-call | tf_op jit(solution)/shard_map/cluster_exchange/pallas_call | solution.py:697
  72.6 0.6 spill.1

commit v7 on v6

--- a/solution.py
+++ b/solution.py
@@ -621,7 +621,7 @@
         found = mm(wanted, members)
         for t in range(R):
             finish(t, found[:, t * CK : (t + 1) * CK])
-        for t in [5, 3, 7, 6, 4, 2, 1, 0] if R == 8 else range(R):
+        for t in [5, 3, 4, 2, 7, 6, 1, 0] if R == 8 else range(R):
             deliver(t)
     else:
 

time: 73.4 us -> 73.4 us (level)
  no operation moved by 1% of the time
where the time goes in v7:
time: 73.4 us; the launch traced here: 73.2 us
  Pallas kernels  72.6 us (99%)
    pallas_call x1, Pallas kernels, local(): pl.pallas_call(functools.partial(kernel, (R, C, K, Q, cuts, straight)), n...  72 us

profile of v7, /device:TPU:0, one launch (start us, length us, event | category | flops | bytes accessed | tf_op | source)
XLA Modules:
  0.0 73.2 jit_solution(3862035732366021794)
XLA Ops:
  0.6 72.0 %cluster_exchange.1.packed_ref = f32[8,512]{1,0:T(8,128)S(1)} custom-call(bf16[512,2048]{1,0:T(8,128)(2,1)} %docs_hbm.1, s32[1,512]{1,0:T(1,128)} %bitcast.5, bf16[384,2048]{1,0:T(8,128)(2,1)} %cent_hbm.1, s32[96,128]{1,0:T(8,128)} %bitcast.4), custom_call_target="tpu_custom_call" | custom-call | tf_op jit(solution)/shard_map/cluster_exchange/pallas_call | solution.py:697
  72.6 0.6 spill.1
